TPU v7x, 256 devices: a whole 4x4x8 slice. The times are simulated.
256 devices in a mesh: gx: 8 (over z), gy: 4 (over x_lo, core), gz: 8 (over y, x_hi).
Axes of the slice: x: 4 (x_hi: 2, x_lo: 2; x = x_hi * 2 + x_lo), y: 4, z: 8, core: 2. Of those that a mesh axis runs over, the one named last changes fastest.
Arguments:
- source: float32 [128, 128, 512], P('gx', 'gz', 'gy'), may hold values from -0.6 to 0.6
- shift: float32 [1], replicated, may hold values from 1e-05 to 0.0001
Outputs:
- solution: float32 [128, 128, 512], P('gx', 'gz', 'gy')
All inputs are finite; a program needn't handle non-finite values.
Results may differ from a plain program's by a relative error of at most 0.0004.
Values sent between devices are 32-bit elements; how exact they have to be, the bound alone decides.
A program may use at most 64 MiB of HBM per device.

v0:
```python
import math

import jax
import jax.numpy as jnp
from jax import lax
from jax.sharding import Mesh
from jax.sharding import PartitionSpec as P

LEVELS = 4
GX_GY_GZ = ("gx", "gy_0", "gy_1", "gz_0", "gz_1")
GY = ("gy_0", "gy_1")
GZ = ("gz_0", "gz_1")


DAMPING = 6.0 / 7.0
PRECISE = lax.Precision.HIGHEST
CUBIC_EVEN = (-5.0 / 128.0, 35.0 / 128.0, 105.0 / 128.0, -7.0 / 128.0)
CUBIC_ODD = (-7.0 / 128.0, 105.0 / 128.0, 35.0 / 128.0, -5.0 / 128.0)
LINEAR_EVEN = (0.25, 0.75)
LINEAR_ODD = (0.75, 0.25)


def cut_rows(length, count):
    lap = length // count
    if lap >= 8:
        lap -= lap % 8
    return [lap * k for k in range(1, count)]


def gather_in_order(array, axes, turns):
    blocks = array
    for k in turns:
        blocks = lax.all_gather(blocks, axes[k])
    done = turns[::-1]
    back = [done.index(k) for k in range(len(axes))]
    blocks = blocks.transpose(*back, *range(len(axes), blocks.ndim))
    return blocks.reshape(-1, *array.shape)


def laid_out(blocks, dim):
    blocks = jnp.moveaxis(blocks, 0, dim)
    dims = blocks.shape
    return blocks.reshape(*dims[:dim], dims[dim] * dims[dim + 1], *dims[dim + 2 :])


def gather_at_once(array, axes, dim):
    cut = max(range(max(1, array.ndim - 1)), key=lambda d: array.shape[d])
    count, done = (len(axes), [])
    for initial, share in enumerate(jnp.split(array, cut_rows(array.shape[cut], count), axis=cut)):
        if share.size:
            turns = [(initial - k) % count for k in range(count)]
            done.append(gather_in_order(share, axes, turns))
    return laid_out(jnp.concatenate(done, axis=cut + 1), dim)


def with_halo(array, sides, width):
    edges = {}
    for axis, dim in sides:
        size, length = (lax.axis_size(axis), array.shape[dim])
        up = [(i, (i + 1) % size) for i in range(size)]
        last = lax.slice_in_dim(array, length - width, length, axis=dim)
        initial = lax.slice_in_dim(array, 0, width, axis=dim)
        edges[dim] = (
            lax.ppermute(last, axis, up),
            lax.ppermute(initial, axis, [(b, a) for a, b in up]),
        )
    done = []
    for _, dim in sides:
        low, high = edges[dim]
        around = [(width, width) if d in done else (0, 0) for d in range(array.ndim)]
        array = jnp.concatenate([jnp.pad(low, around), array, jnp.pad(high, around)], axis=dim)
        done.append(dim)
    return array


def extended(block, sides, width):
    for axis, dim in sides:
        count = lax.axis_size(axis)
        forward = [(i, i + 1) for i in range(count - 1)]
        forward.append((count - 1, 0))
        backward = [(target, source) for source, target in forward]
        low = lax.ppermute(
            lax.slice_in_dim(block, block.shape[dim] - width, None, axis=dim), axis, forward
        )
        high = lax.ppermute(lax.slice_in_dim(block, 0, width, axis=dim), axis, backward)
        block = jnp.concatenate([low, block, high], axis=dim)
    return block


def wrapped(values, width):
    return jnp.pad(values, width, mode="wrap")


def neighbours(padded):
    center = padded[1:-1, 1:-1, 1:-1]
    beside_all = padded[2:, 1:-1, 1:-1] + padded[:-2, 1:-1, 1:-1]
    beside_all = beside_all + padded[1:-1, 2:, 1:-1] + padded[1:-1, :-2, 1:-1]
    beside_all = beside_all + padded[1:-1, 1:-1, 2:] + padded[1:-1, 1:-1, :-2]
    return (center, beside_all)


def defect(padded, forcing, weight_nb, diagonal):
    center, beside_all = neighbours(padded)
    return forcing - (diagonal * center - weight_nb * beside_all)


def relaxed(padded, forcing, weight_nb, diagonal):
    center, beside_all = neighbours(padded)
    return center + DAMPING * (forcing - (diagonal * center - weight_nb * beside_all)) / diagonal


def coarsen(values):
    values = values[0::2] + values[1::2]
    values = values[:, 0::2] + values[:, 1::2]
    values = values[:, :, 0::2] + values[:, :, 1::2]
    return 0.125 * values


def refine_axis(padded, dimension, even_weights, odd_weights):
    margin = len(even_weights) // 2
    length = padded.shape[dimension] - 2 * margin
    even_cells = even_weights[0] * lax.slice_in_dim(padded, 0, length, axis=dimension)
    odd_cells = odd_weights[0] * lax.slice_in_dim(padded, 1, 1 + length, axis=dimension)
    for offset in range(1, len(even_weights)):
        even_cells = even_cells + even_weights[offset] * lax.slice_in_dim(
            padded, offset, offset + length, axis=dimension
        )
        odd_cells = odd_cells + odd_weights[offset] * lax.slice_in_dim(
            padded, offset + 1, offset + 1 + length, axis=dimension
        )
    stacked = jnp.stack([even_cells, odd_cells], axis=dimension + 1)
    new_shape = list(even_cells.shape)
    new_shape[dimension] = 2 * length
    return stacked.reshape(new_shape)


def refine(padded, even_weights, odd_weights):
    for dimension in range(3):
        padded = refine_axis(padded, dimension, even_weights, odd_weights)
    return padded


def tables(cells_count):
    indices = jnp.arange(cells_count, dtype=jnp.int32)
    angles = (indices[:, None] * indices[None, :] % cells_count).astype(jnp.float32) * (
        2.0 * math.pi / cells_count
    )
    return (jnp.cos(angles), jnp.sin(angles))


def along_axis(matrix, values, dimension):
    product = jnp.tensordot(matrix, values, axes=([1], [dimension]), precision=PRECISE)
    return jnp.moveaxis(product, 0, dimension)


def coarse_solve(forcing, shift_value, weight_nb):
    cosine_table, sine_table = tables(forcing.shape[0])
    real_part = along_axis(cosine_table, forcing, 0)
    imag_part = -along_axis(sine_table, forcing, 0)
    for dimension in (1, 2):
        cosine_table, sine_table = tables(forcing.shape[dimension])
        real_next = along_axis(cosine_table, real_part, dimension) + along_axis(
            sine_table, imag_part, dimension
        )
        imag_part = along_axis(cosine_table, imag_part, dimension) - along_axis(
            sine_table, real_part, dimension
        )
        real_part = real_next
    cosines = [
        jnp.cos(jnp.arange(cells_count, dtype=jnp.float32) * (2.0 * math.pi / cells_count))
        for cells_count in forcing.shape
    ]
    eigenvalue = (
        weight_nb
        * (
            6.0
            - 2.0 * cosines[0][:, None, None]
            - 2.0 * cosines[1][None, :, None]
            - 2.0 * cosines[2][None, None, :]
        )
        + shift_value
    )
    real_part = real_part / eigenvalue
    imag_part = imag_part / eigenvalue
    for dimension in (0, 1):
        cosine_table, sine_table = tables(forcing.shape[dimension])
        real_next = along_axis(cosine_table, real_part, dimension) - along_axis(
            sine_table, imag_part, dimension
        )
        imag_part = along_axis(cosine_table, imag_part, dimension) + along_axis(
            sine_table, real_part, dimension
        )
        real_part = real_next
    cosine_table, sine_table = tables(forcing.shape[2])
    real_part = along_axis(cosine_table, real_part, 2) - along_axis(sine_table, imag_part, 2)
    return real_part / float(forcing.size)


def vcycle_whole(grid_level, iterate, forcing, shift_value):
    weight_nb = 0.25**grid_level
    diagonal = 6.0 * weight_nb + shift_value
    iterate = relaxed(wrapped(iterate, 1), forcing, weight_nb, diagonal)
    residue = coarsen(defect(wrapped(iterate, 1), forcing, weight_nb, diagonal))
    correction = coarse_solve(residue, shift_value, 0.25 ** (grid_level + 1))
    iterate = iterate + refine(wrapped(correction, 1), LINEAR_EVEN, LINEAR_ODD)
    iterate = relaxed(wrapped(iterate, 1), forcing, weight_nb, diagonal)
    return iterate


def collect(block):
    gathered = gather_at_once(block[None], GX_GY_GZ, 0)
    devices_first = lax.axis_size("gx")
    devices_third = lax.axis_size(GY)
    devices_second = lax.axis_size(GZ)
    extent_first, extent_second, extent_third = block.shape
    gathered = gathered.reshape(
        devices_first, devices_third, devices_second, extent_first, extent_second, extent_third
    )
    gathered = jnp.transpose(gathered, (0, 3, 2, 4, 1, 5))
    return gathered.reshape(
        devices_first * extent_first, devices_second * extent_second, devices_third * extent_third
    )


def own_block(whole, width, block_shape):
    padded = jnp.pad(whole, width, mode="wrap")
    starts = (
        lax.axis_index("gx") * block_shape[0],
        lax.axis_index(GZ) * block_shape[1],
        lax.axis_index(GY) * block_shape[2],
    )
    extents = (block_shape[0] + 2 * width, block_shape[1] + 2 * width, block_shape[2] + 2 * width)
    return lax.dynamic_slice(padded, starts, extents)


def faces(iterate):
    return with_halo(iterate, (("gx", 0), (GY, 2), (GZ, 1)), 1)


def smooth_each(iterate, forcing, weight_nb, diagonal, zero_start):
    if zero_start:
        iterate = DAMPING * forcing / diagonal
    else:
        iterate = relaxed(faces(iterate), forcing, weight_nb, diagonal)
    return iterate


def vcycle_split(grid_level, iterate, forcing, shift_value, zero_start, gather_level):
    weight_nb = 0.25**grid_level
    diagonal = 6.0 * weight_nb + shift_value
    iterate = smooth_each(iterate, forcing, weight_nb, diagonal, zero_start)
    residue = defect(faces(iterate), forcing, weight_nb, diagonal)
    coarse_residue = coarsen(residue)
    if grid_level + 1 < gather_level:
        correction = vcycle_split(
            grid_level + 1, None, coarse_residue, shift_value, True, gather_level
        )
        rim = extended(correction, (("gx", 0), (GY, 2), (GZ, 1)), 1)
    else:
        whole_residue = collect(coarse_residue)
        whole_correction = vcycle_whole(
            gather_level, jnp.zeros_like(whole_residue), whole_residue, shift_value
        )
        rim = own_block(whole_correction, 1, coarse_residue.shape)
    iterate = iterate + refine(rim, LINEAR_EVEN, LINEAR_ODD)
    iterate = smooth_each(iterate, forcing, weight_nb, diagonal, False)
    return iterate


def per_device(source, shift):
    shift_value = shift[0]
    gather_level = LEVELS - 2
    sources = [source]
    for grid_level in range(1, gather_level + 1):
        sources.append(coarsen(sources[-1]))
    whole_sources = [collect(sources[gather_level])]
    whole_sources.append(coarsen(whole_sources[-1]))
    whole = coarse_solve(whole_sources[-1], shift_value, 0.25 ** (LEVELS - 1))
    grid_level = 2
    whole = refine(wrapped(whole, 2), CUBIC_EVEN, CUBIC_ODD)
    whole = vcycle_whole(grid_level, whole, whole_sources[grid_level - gather_level], shift_value)
    iterate = None
    for grid_level in range(gather_level - 1, -1, -1):
        if grid_level == gather_level - 1:
            rim = own_block(whole, 2, sources[grid_level + 1].shape)
        else:
            rim = extended(iterate, (("gx", 0), (GY, 2), (GZ, 1)), 2)
        iterate = refine(rim, CUBIC_EVEN, CUBIC_ODD)
        iterate = vcycle_split(
            grid_level, iterate, sources[grid_level], shift_value, False, gather_level
        )
    return iterate


def solution(mesh):
    split = Mesh(
        mesh.devices.reshape(mesh.shape["gx"], 2, 2, 4, 2), ("gx", "gy_0", "gy_1", "gz_0", "gz_1")
    )
    placed = (P("gx", GZ, GY), P())
    return jax.shard_map(
        per_device, mesh=split, in_specs=placed, out_specs=P("gx", GZ, GY), check_vma=False
    )
```

profile of v0, /device:TPU:1, one launch (start us, length us, event | category | flops | bytes accessed | tf_op | source)
XLA Modules:
  0.0 444.5 jit_solution(9244354609529318937)
XLA Ops:
  2.6 5.3 %all-gather = f32[8,4,32]{2,1,0:T(4,128)S(1)} all-gather(f32[4,4,32]{2,1,0:T(4,128)S(1)} %add_multiply_fusion.7), channel_id=2, replica_groups=mesh['gx'=8,'gy_0'=2,'gy_1'=2,'gz_0'=4,'gz_1'=2] {'gz_1'}, dimensions={0}, use_global_device_ids=true | all-gather | bytes 6144 | tf_op jit(solution)/shard_map/all_gather | solution.py:33
  7.9 9.7 %all-gather.1 = f32[8,1,4,4,32]{4,2,0,3,1:T(4,128)S(1)} all-gather(f32[2,1,4,4,32]{4,2,0,3,1:T(4,128)S(1)} %bitcast.452), channel_id=3, replica_groups=mesh['gx'=8,'gy_0'=2,'gy_1'=2,'gz_0'=4,'gz_1'=2] {'gz_0'}, dimensions={0}, use_global_device_ids=true | all-gather | bytes 20480 | tf_op jit(solution)/shard_map/all_gather | solution.py:33
  17.6 7.4 %all-gather.2 = f32[8,2,1,4,4,32]{5,1,0,4,3,2:T(2,128)S(1)} all-gather(f32[4,2,1,4,4,32]{5,1,0,4,3,2:T(2,128)S(1)} %bitcast.443), channel_id=4, replica_groups=mesh['gx'=8,'gy_0'=2,'gy_1'=2,'gz_0'=4,'gz_1'=2] {'gy_1'}, dimensions={0}, use_global_device_ids=true | all-gather | bytes 49152 | tf_op jit(solution)/shard_map/all_gather | solution.py:33
  25.0 5.4 %all-gather.3 = f32[4,4,2,1,4,4,32]{6,1,0,5,4,2,3:T(4,128)S(1)} all-gather(f32[2,4,2,1,4,4,32]{6,1,0,5,4,2,3:T(4,128)S(1)} %bitcast.437), channel_id=5, replica_groups=mesh['gx'=8,'gy_0'=2,'gy_1'=2,'gz_0'=4,'gz_1'=2] {'gy_0'}, dimensions={0}, use_global_device_ids=true | all-gather | bytes 98304 | tf_op jit(solution)/shard_map/all_gather | solution.py:33
  30.5 27.1 %all-gather.4 = f32[16,2,4,2,1,4,4,32]{7,6,5,4,3,2,1,0:T(4,128)S(1)} all-gather(f32[2,2,4,2,1,4,4,32]{7,6,5,4,3,2,1,0:T(4,128)S(1)} %copy.1539), channel_id=6, replica_groups=mesh['gx'=8,'gy_0'=2,'gy_1'=2,'gz_0'=4,'gz_1'=2] {'gx'}, dimensions={0}, use_global_device_ids=true | all-gather | bytes 589824 | tf_op jit(solution)/shard_map/all_gather | solution.py:33
  110.3 6.9 %collective-permute-start.2 = (f32[8,8,1]{2,1,0:T(8,128)S(1)}, f32[8,8,1]{2,1,0:T(8,128)S(1)}, u32[]{:S(2)}, u32[]{:S(2)}) collective-permute-start(f32[8,8,1]{2,1,0:T(8,128)S(1)} %get-tuple-element.194), channel_id=1, source_target_pairs={{0,8},{8,16},{16,24},{24,0},{1,9},{9,17},{17,25},{25,1},{2,10},{10... | collective-permute-start | bytes 776 | tf_op jit(solution)/shard_map/ppermute | solution.py:64
  122.4 5.5 %collective-permute-done.5 = f32[8,1,64]{2,1,0:T(1,128)S(1)} collective-permute-done((f32[8,1,64]{2,1,0:T(1,128)S(1)}, f32[8,1,64]{2,1,0:T(1,128)S(1)}, u32[]{:S(2)}, u32[]{:S(2)}) %collective-permute-start.5) | collective-permute-done | bytes 2080 | tf_op jit(solution)/shard_map/ppermute | solution.py:64
  142.1 4.7 %all-gather.5 = f32[8,4,32]{2,1,0:T(4,128)S(1)} all-gather(f32[4,4,32]{2,1,0:T(4,128)S(1)} %add_multiply_fusion.6), channel_id=7, replica_groups=mesh['gx'=8,'gy_0'=2,'gy_1'=2,'gz_0'=4,'gz_1'=2] {'gz_1'}, dimensions={0}, use_global_device_ids=true | all-gather | bytes 6144 | tf_op jit(solution)/shard_map/all_gather | solution.py:33
  146.8 9.0 %all-gather.6 = f32[8,1,4,4,32]{4,3,2,1,0:T(4,128)S(1)} all-gather(f32[2,1,4,4,32]{4,3,2,1,0:T(4,128)S(1)} %bitcast.453), channel_id=8, replica_groups=mesh['gx'=8,'gy_0'=2,'gy_1'=2,'gz_0'=4,'gz_1'=2] {'gz_0'}, dimensions={0}, use_global_device_ids=true | all-gather | bytes 20480 | tf_op jit(solution)/shard_map/all_gather | solution.py:33
  155.8 6.1 %all-gather.7 = f32[8,2,1,4,4,32]{5,1,0,4,3,2:T(2,128)S(1)} all-gather(f32[4,2,1,4,4,32]{5,1,0,4,3,2:T(2,128)S(1)} %bitcast.446), channel_id=9, replica_groups=mesh['gx'=8,'gy_0'=2,'gy_1'=2,'gz_0'=4,'gz_1'=2] {'gy_1'}, dimensions={0}, use_global_device_ids=true | all-gather | bytes 49152 | tf_op jit(solution)/shard_map/all_gather | solution.py:33
  162.0 5.4 %all-gather.8 = f32[4,4,2,1,4,4,32]{6,1,0,5,4,2,3:T(4,128)S(1)} all-gather(f32[2,4,2,1,4,4,32]{6,1,0,5,4,2,3:T(4,128)S(1)} %bitcast.438), channel_id=10, replica_groups=mesh['gx'=8,'gy_0'=2,'gy_1'=2,'gz_0'=4,'gz_1'=2] {'gy_0'}, dimensions={0}, use_global_device_ids=true | all-gather | bytes 98304 | tf_op jit(solution)/shard_map/all_gather | solution.py:33
  167.4 25.5 %all-gather.9 = f32[16,2,4,2,1,4,4,32]{7,6,5,4,3,2,1,0:T(4,128)S(1)} all-gather(f32[2,2,4,2,1,4,4,32]{7,6,5,4,3,2,1,0:T(4,128)S(1)} %copy.1613), channel_id=11, replica_groups=mesh['gx'=8,'gy_0'=2,'gy_1'=2,'gz_0'=4,'gz_1'=2] {'gx'}, dimensions={0}, use_global_device_ids=true | all-gather | bytes 589824 | tf_op jit(solution)/shard_map/all_gather | solution.py:33
  228.1 6.5 %collective-permute-start.14 = (f32[8,8,1]{2,1,0:T(8,128)S(1)}, f32[8,8,1]{2,1,0:T(8,128)S(1)}, u32[]{:S(2)}, u32[]{:S(2)}) collective-permute-start(f32[8,8,1]{2,1,0:T(8,128)S(1)} %get-tuple-element.180), channel_id=1, source_target_pairs={{0,8},{8,16},{16,24},{24,0},{1,9},{9,17},{17,25},{25,1},{2,10},{10... | collective-permute-start | bytes 776 | tf_op jit(solution)/shard_map/ppermute | solution.py:64
  249.7 4.9 %collective-permute-start.23 = (f32[12,2,68]{2,1,0:T(2,128)S(1)}, f32[12,2,68]{2,1,0:T(2,128)S(1)}, u32[]{:S(2)}, u32[]{:S(2)}) collective-permute-start(f32[12,2,68]{2,1,0:T(2,128)S(1)} %get-tuple-element.112), channel_id=1, source_target_pairs={{1,0},{2,1},{3,2},{4,3},{5,4},{6,5},{7,6},{0,7},{9,8},{10,9},{11,1... | collective-permute-start | bytes 19592 | tf_op jit(solution)/shard_map/ppermute | solution.py:85
  258.5 5.1 %collective-permute-start.28 = (f32[16,1,128]{2,0,1:T(8,128)S(1)}, f32[16,1,128]{2,0,1:T(8,128)S(1)}, u32[]{:S(2)}, u32[]{:S(2)}) collective-permute-start(f32[16,1,128]{2,0,1:T(8,128)S(1)} %copy.1657), channel_id=1, source_target_pairs={{1,0},{2,1},{3,2},{4,3},{5,4},{6,5},{7,6},{0,7},{9,8},{10,9},{11,1... | collective-permute-start | bytes 24584 | tf_op jit(solution)/shard_map/ppermute | solution.py:65
  277.1 6.0 %collective-permute-start.34 = (f32[16,1,128]{2,0,1:T(8,128)S(1)}, f32[16,1,128]{2,0,1:T(8,128)S(1)}, u32[]{:S(2)}, u32[]{:S(2)}) collective-permute-start(f32[16,1,128]{2,0,1:T(8,128)S(1)} %bitcast.466), channel_id=1, source_target_pairs={{1,0},{2,1},{3,2},{4,3},{5,4},{6,5},{7,6},{0,7},{9,8},{10,9},{11,1... | collective-permute-start | bytes 24584 | tf_op jit(solution)/shard_map/ppermute | solution.py:65
  297.8 6.0 %collective-permute-start.40 = (f32[8,1,64]{2,1,0:T(1,128)S(1)}, f32[8,1,64]{2,1,0:T(1,128)S(1)}, u32[]{:S(2)}, u32[]{:S(2)}) collective-permute-start(f32[8,1,64]{2,1,0:T(1,128)S(1)} %get-tuple-element.169), channel_id=1, source_target_pairs={{1,0},{2,1},{3,2},{4,3},{5,4},{6,5},{7,6},{0,7},{9,8},{10,9},{11,1... | collective-permute-start | bytes 6152 | tf_op jit(solution)/shard_map/ppermute | solution.py:65
  315.1 9.3 %all-gather.11 = f32[8,1,4,4,32]{4,3,2,1,0:T(4,128)S(1)} all-gather(f32[2,1,4,4,32]{4,3,2,1,0:T(4,128)S(1)} %bitcast.454), channel_id=13, replica_groups=mesh['gx'=8,'gy_0'=2,'gy_1'=2,'gz_0'=4,'gz_1'=2] {'gz_0'}, dimensions={0}, use_global_device_ids=true | all-gather | bytes 20480 | tf_op jit(solution)/shard_map/all_gather | solution.py:33
  324.4 6.8 %all-gather.12 = f32[8,2,1,4,4,32]{5,1,0,4,3,2:T(2,128)S(1)} all-gather(f32[4,2,1,4,4,32]{5,1,0,4,3,2:T(2,128)S(1)} %bitcast.447), channel_id=14, replica_groups=mesh['gx'=8,'gy_0'=2,'gy_1'=2,'gz_0'=4,'gz_1'=2] {'gy_1'}, dimensions={0}, use_global_device_ids=true | all-gather | bytes 49152 | tf_op jit(solution)/shard_map/all_gather | solution.py:33
  331.2 5.4 %all-gather.13 = f32[4,4,2,1,4,4,32]{6,1,0,5,4,2,3:T(4,128)S(1)} all-gather(f32[2,4,2,1,4,4,32]{6,1,0,5,4,2,3:T(4,128)S(1)} %bitcast.439), channel_id=15, replica_groups=mesh['gx'=8,'gy_0'=2,'gy_1'=2,'gz_0'=4,'gz_1'=2] {'gy_0'}, dimensions={0}, use_global_device_ids=true | all-gather | bytes 98304 | tf_op jit(solution)/shard_map/all_gather | solution.py:33
  336.7 24.9 %all-gather.14 = f32[16,2,4,2,1,4,4,32]{7,6,5,4,3,2,1,0:T(4,128)S(1)} all-gather(f32[2,2,4,2,1,4,4,32]{7,6,5,4,3,2,1,0:T(4,128)S(1)} %copy.1669), channel_id=16, replica_groups=mesh['gx'=8,'gy_0'=2,'gy_1'=2,'gz_0'=4,'gz_1'=2] {'gx'}, dimensions={0}, use_global_device_ids=true | all-gather | bytes 589824 | tf_op jit(solution)/shard_map/all_gather | solution.py:33
  397.0 5.5 %collective-permute-start.44 = (f32[8,8,1]{2,1,0:T(8,128)S(1)}, f32[8,8,1]{2,1,0:T(8,128)S(1)}, u32[]{:S(2)}, u32[]{:S(2)}) collective-permute-start(f32[8,8,1]{2,1,0:T(8,128)S(1)} %get-tuple-element.164), channel_id=1, source_target_pairs={{0,8},{8,16},{16,24},{24,0},{1,9},{9,17},{17,25},{25,1},{2,10},{10... | collective-permute-start | bytes 776 | tf_op jit(solution)/shard_map/ppermute | solution.py:64
  418.5 5.1 %collective-permute-start.53 = (f32[10,1,66]{2,1,0:T(1,128)S(1)}, f32[10,1,66]{2,1,0:T(1,128)S(1)}, u32[]{:S(2)}, u32[]{:S(2)}) collective-permute-start(f32[10,1,66]{2,1,0:T(1,128)S(1)} %get-tuple-element.144), channel_id=1, source_target_pairs={{1,0},{2,1},{3,2},{4,3},{5,4},{6,5},{7,6},{0,7},{9,8},{10,9},{11,1... | collective-permute-start | bytes 7928 | tf_op jit(solution)/shard_map/ppermute | solution.py:85
  426.4 5.2 %collective-permute-start.58 = (f32[16,1,128]{2,0,1:T(8,128)S(1)}, f32[16,1,128]{2,0,1:T(8,128)S(1)}, u32[]{:S(2)}, u32[]{:S(2)}) collective-permute-start(f32[16,1,128]{2,0,1:T(8,128)S(1)} %bitcast.465), channel_id=1, source_target_pairs={{1,0},{2,1},{3,2},{4,3},{5,4},{6,5},{7,6},{0,7},{9,8},{10,9},{11,1... | collective-permute-start | bytes 24584 | tf_op jit(solution)/shard_map/ppermute | solution.py:65
  (529 shorter events, 232.3 us)
Async XLA Ops:
  107.0 15.0 %collective-permute-start = (f32[1,8,64]{1,2,0:T(8,128)S(1)}, f32[1,8,64]{1,2,0:T(8,128)S(1)}, u32[]{:S(2)}, u32[]{:S(2)}) collective-permute-start(f32[1,8,64]{1,2,0:T(8,128)S(1)} %bitcast.455), channel_id=1, source_target_pairs={{32,0},{64,32},{96,64},{128,96},{160,128},{192,160},{224,192},{0,2... | collective-permute-start | bytes 6152 | tf_op jit(solution)/shard_map/ppermute | solution.py:65
  109.6 12.4 %collective-permute-start.1 = (f32[1,8,64]{1,2,0:T(8,128)S(1)}, f32[1,8,64]{1,2,0:T(8,128)S(1)}, u32[]{:S(2)}, u32[]{:S(2)}) collective-permute-start(f32[1,8,64]{1,2,0:T(8,128)S(1)} %bitcast.456), channel_id=1, source_target_pairs={{0,32},{32,64},{64,96},{96,128},{128,160},{160,192},{192,224},{224... | collective-permute-start | bytes 6152 | tf_op jit(solution)/shard_map/ppermute | solution.py:64
  110.3 11.4 %collective-permute-start.2 = (f32[8,8,1]{2,1,0:T(8,128)S(1)}, f32[8,8,1]{2,1,0:T(8,128)S(1)}, u32[]{:S(2)}, u32[]{:S(2)}) collective-permute-start(f32[8,8,1]{2,1,0:T(8,128)S(1)} %get-tuple-element.194), channel_id=1, source_target_pairs={{0,8},{8,16},{16,24},{24,0},{1,9},{9,17},{17,25},{25,1},{2,10},{10... | collective-permute-start | bytes 776 | tf_op jit(solution)/shard_map/ppermute | solution.py:64
  130.7 10.9 %collective-permute-start.10 = (f32[8,1,64]{2,1,0:T(1,128)S(1)}, f32[8,1,64]{2,1,0:T(1,128)S(1)}, u32[]{:S(2)}, u32[]{:S(2)}) collective-permute-start(f32[8,1,64]{2,1,0:T(1,128)S(1)} %get-tuple-element.185), channel_id=1, source_target_pairs={{1,0},{2,1},{3,2},{4,3},{5,4},{6,5},{7,6},{0,7},{9,8},{10,9},{11,1... | collective-permute-start | bytes 6152 | tf_op jit(solution)/shard_map/ppermute | solution.py:65
  130.8 10.7 %collective-permute-start.11 = (f32[8,1,64]{2,1,0:T(1,128)S(1)}, f32[8,1,64]{2,1,0:T(1,128)S(1)}, u32[]{:S(2)}, u32[]{:S(2)}) collective-permute-start(f32[8,1,64]{2,1,0:T(1,128)S(1)} %get-tuple-element.186), channel_id=1, source_target_pairs={{0,1},{1,2},{2,3},{3,4},{4,5},{5,6},{6,7},{7,0},{8,9},{9,10},{10,1... | collective-permute-start | bytes 6152 | tf_op jit(solution)/shard_map/ppermute | solution.py:64
  222.5 17.3 %collective-permute-start.12 = (f32[1,8,64]{2,1,0:T(8,128)S(1)}, f32[1,8,64]{2,1,0:T(8,128)S(1)}, u32[]{:S(2)}, u32[]{:S(2)}) collective-permute-start(f32[1,8,64]{2,1,0:T(8,128)S(1)} %get-tuple-element.182), channel_id=1, source_target_pairs={{32,0},{64,32},{96,64},{128,96},{160,128},{192,160},{224,192},{0,2... | collective-permute-start | bytes 6152 | tf_op jit(solution)/shard_map/ppermute | solution.py:65
  224.5 15.3 %collective-permute-start.13 = (f32[1,8,64]{2,1,0:T(8,128)S(1)}, f32[1,8,64]{2,1,0:T(8,128)S(1)}, u32[]{:S(2)}, u32[]{:S(2)}) collective-permute-start(f32[1,8,64]{2,1,0:T(8,128)S(1)} %get-tuple-element.181), channel_id=1, source_target_pairs={{0,32},{32,64},{64,96},{96,128},{128,160},{160,192},{192,224},{224... | collective-permute-start | bytes 6152 | tf_op jit(solution)/shard_map/ppermute | solution.py:64
  224.9 14.9 %collective-permute-start.16 = (f32[8,1,64]{2,1,0:T(1,128)S(1)}, f32[8,1,64]{2,1,0:T(1,128)S(1)}, u32[]{:S(2)}, u32[]{:S(2)}) collective-permute-start(f32[8,1,64]{2,1,0:T(1,128)S(1)} %get-tuple-element.177), channel_id=1, source_target_pairs={{1,0},{2,1},{3,2},{4,3},{5,4},{6,5},{7,6},{0,7},{9,8},{10,9},{11,1... | collective-permute-start | bytes 6152 | tf_op jit(solution)/shard_map/ppermute | solution.py:65
  227.6 12.3 %collective-permute-start.17 = (f32[8,1,64]{2,1,0:T(1,128)S(1)}, f32[8,1,64]{2,1,0:T(1,128)S(1)}, u32[]{:S(2)}, u32[]{:S(2)}) collective-permute-start(f32[8,1,64]{2,1,0:T(1,128)S(1)} %get-tuple-element.178), channel_id=1, source_target_pairs={{0,1},{1,2},{2,3},{3,4},{4,5},{5,6},{6,7},{7,0},{8,9},{9,10},{10,1... | collective-permute-start | bytes 6152 | tf_op jit(solution)/shard_map/ppermute | solution.py:64
  258.5 18.3 %collective-permute-start.28 = (f32[16,1,128]{2,0,1:T(8,128)S(1)}, f32[16,1,128]{2,0,1:T(8,128)S(1)}, u32[]{:S(2)}, u32[]{:S(2)}) collective-permute-start(f32[16,1,128]{2,0,1:T(8,128)S(1)} %copy.1657), channel_id=1, source_target_pairs={{1,0},{2,1},{3,2},{4,3},{5,4},{6,5},{7,6},{0,7},{9,8},{10,9},{11,1... | collective-permute-start | bytes 24584 | tf_op jit(solution)/shard_map/ppermute | solution.py:65
  264.0 12.8 %collective-permute-start.29 = (f32[16,1,128]{2,0,1:T(8,128)S(1)}, f32[16,1,128]{2,0,1:T(8,128)S(1)}, u32[]{:S(2)}, u32[]{:S(2)}) collective-permute-start(f32[16,1,128]{2,0,1:T(8,128)S(1)} %copy.1659), channel_id=1, source_target_pairs={{0,1},{1,2},{2,3},{3,4},{4,5},{5,6},{6,7},{7,0},{8,9},{9,10},{10,1... | collective-permute-start | bytes 24584 | tf_op jit(solution)/shard_map/ppermute | solution.py:64
  264.2 12.5 %collective-permute-start.24 = (f32[1,16,128]{1,2,0:T(8,128)S(1)}, f32[1,16,128]{1,2,0:T(8,128)S(1)}, u32[]{:S(2)}, u32[]{:S(2)}) collective-permute-start(f32[1,16,128]{1,2,0:T(8,128)S(1)} %bitcast.450), channel_id=1, source_target_pairs={{32,0},{64,32},{96,64},{128,96},{160,128},{192,160},{224,192},{0,2... | collective-permute-start | bytes 24584 | tf_op jit(solution)/shard_map/ppermute | solution.py:65
  277.1 16.2 %collective-permute-start.34 = (f32[16,1,128]{2,0,1:T(8,128)S(1)}, f32[16,1,128]{2,0,1:T(8,128)S(1)}, u32[]{:S(2)}, u32[]{:S(2)}) collective-permute-start(f32[16,1,128]{2,0,1:T(8,128)S(1)} %bitcast.466), channel_id=1, source_target_pairs={{1,0},{2,1},{3,2},{4,3},{5,4},{6,5},{7,6},{0,7},{9,8},{10,9},{11,1... | collective-permute-start | bytes 24584 | tf_op jit(solution)/shard_map/ppermute | solution.py:65
  283.1 10.2 %collective-permute-start.30 = (f32[1,16,128]{2,1,0:T(8,128)S(1)}, f32[1,16,128]{2,1,0:T(8,128)S(1)}, u32[]{:S(2)}, u32[]{:S(2)}) collective-permute-start(f32[1,16,128]{2,1,0:T(8,128)S(1)} %get-tuple-element.132), channel_id=1, source_target_pairs={{32,0},{64,32},{96,64},{128,96},{160,128},{192,160},{224,192},{0,2... | collective-permute-start | bytes 24584 | tf_op jit(solution)/shard_map/ppermute | solution.py:65
  294.9 14.5 %collective-permute-start.36 = (f32[1,8,64]{2,1,0:T(8,128)S(1)}, f32[1,8,64]{2,1,0:T(8,128)S(1)}, u32[]{:S(2)}, u32[]{:S(2)}) collective-permute-start(f32[1,8,64]{2,1,0:T(8,128)S(1)} %get-tuple-element.174), channel_id=1, source_target_pairs={{32,0},{64,32},{96,64},{128,96},{160,128},{192,160},{224,192},{0,2... | collective-permute-start | bytes 6152 | tf_op jit(solution)/shard_map/ppermute | solution.py:65
  297.8 11.6 %collective-permute-start.37 = (f32[1,8,64]{2,1,0:T(8,128)S(1)}, f32[1,8,64]{2,1,0:T(8,128)S(1)}, u32[]{:S(2)}, u32[]{:S(2)}) collective-permute-start(f32[1,8,64]{2,1,0:T(8,128)S(1)} %get-tuple-element.173), channel_id=1, source_target_pairs={{0,32},{32,64},{64,96},{96,128},{128,160},{160,192},{192,224},{224... | collective-permute-start | bytes 6152 | tf_op jit(solution)/shard_map/ppermute | solution.py:64
  297.8 11.6 %collective-permute-start.40 = (f32[8,1,64]{2,1,0:T(1,128)S(1)}, f32[8,1,64]{2,1,0:T(1,128)S(1)}, u32[]{:S(2)}, u32[]{:S(2)}) collective-permute-start(f32[8,1,64]{2,1,0:T(1,128)S(1)} %get-tuple-element.169), channel_id=1, source_target_pairs={{1,0},{2,1},{3,2},{4,3},{5,4},{6,5},{7,6},{0,7},{9,8},{10,9},{11,1... | collective-permute-start | bytes 6152 | tf_op jit(solution)/shard_map/ppermute | solution.py:65
  389.8 18.1 %collective-permute-start.42 = (f32[1,8,64]{2,1,0:T(8,128)S(1)}, f32[1,8,64]{2,1,0:T(8,128)S(1)}, u32[]{:S(2)}, u32[]{:S(2)}) collective-permute-start(f32[1,8,64]{2,1,0:T(8,128)S(1)} %get-tuple-element.166), channel_id=1, source_target_pairs={{32,0},{64,32},{96,64},{128,96},{160,128},{192,160},{224,192},{0,2... | collective-permute-start | bytes 6152 | tf_op jit(solution)/shard_map/ppermute | solution.py:65
  393.2 14.6 %collective-permute-start.43 = (f32[1,8,64]{2,1,0:T(8,128)S(1)}, f32[1,8,64]{2,1,0:T(8,128)S(1)}, u32[]{:S(2)}, u32[]{:S(2)}) collective-permute-start(f32[1,8,64]{2,1,0:T(8,128)S(1)} %get-tuple-element.165), channel_id=1, source_target_pairs={{0,32},{32,64},{64,96},{96,128},{128,160},{160,192},{192,224},{224... | collective-permute-start | bytes 6152 | tf_op jit(solution)/shard_map/ppermute | solution.py:64
  393.4 14.5 %collective-permute-start.46 = (f32[8,1,64]{2,1,0:T(1,128)S(1)}, f32[8,1,64]{2,1,0:T(1,128)S(1)}, u32[]{:S(2)}, u32[]{:S(2)}) collective-permute-start(f32[8,1,64]{2,1,0:T(1,128)S(1)} %get-tuple-element.161), channel_id=1, source_target_pairs={{1,0},{2,1},{3,2},{4,3},{5,4},{6,5},{7,6},{0,7},{9,8},{10,9},{11,1... | collective-permute-start | bytes 6152 | tf_op jit(solution)/shard_map/ppermute | solution.py:65
  396.9 11.0 %collective-permute-start.47 = (f32[8,1,64]{2,1,0:T(1,128)S(1)}, f32[8,1,64]{2,1,0:T(1,128)S(1)}, u32[]{:S(2)}, u32[]{:S(2)}) collective-permute-start(f32[8,1,64]{2,1,0:T(1,128)S(1)} %get-tuple-element.162), channel_id=1, source_target_pairs={{0,1},{1,2},{2,3},{3,4},{4,5},{5,6},{6,7},{7,0},{8,9},{9,10},{10,1... | collective-permute-start | bytes 6152 | tf_op jit(solution)/shard_map/ppermute | solution.py:64
  426.4 17.0 %collective-permute-start.58 = (f32[16,1,128]{2,0,1:T(8,128)S(1)}, f32[16,1,128]{2,0,1:T(8,128)S(1)}, u32[]{:S(2)}, u32[]{:S(2)}) collective-permute-start(f32[16,1,128]{2,0,1:T(8,128)S(1)} %bitcast.465), channel_id=1, source_target_pairs={{1,0},{2,1},{3,2},{4,3},{5,4},{6,5},{7,6},{0,7},{9,8},{10,9},{11,1... | collective-permute-start | bytes 24584 | tf_op jit(solution)/shard_map/ppermute | solution.py:65
  431.6 11.8 %collective-permute-start.59 = (f32[16,1,128]{2,0,1:T(8,128)S(1)}, f32[16,1,128]{2,0,1:T(8,128)S(1)}, u32[]{:S(2)}, u32[]{:S(2)}) collective-permute-start(f32[16,1,128]{2,0,1:T(8,128)S(1)} %bitcast.463), channel_id=1, source_target_pairs={{0,1},{1,2},{2,3},{3,4},{4,5},{5,6},{6,7},{7,0},{8,9},{9,10},{10,1... | collective-permute-start | bytes 24584 | tf_op jit(solution)/shard_map/ppermute | solution.py:64
  431.6 11.8 %collective-permute-start.54 = (f32[1,16,128]{2,1,0:T(8,128)S(1)}, f32[1,16,128]{2,1,0:T(8,128)S(1)}, u32[]{:S(2)}, u32[]{:S(2)}) collective-permute-start(f32[1,16,128]{2,1,0:T(8,128)S(1)} %get-tuple-element.122), channel_id=1, source_target_pairs={{32,0},{64,32},{96,64},{128,96},{160,128},{192,160},{224,192},{0,2... | collective-permute-start | bytes 24584 | tf_op jit(solution)/shard_map/ppermute | solution.py:65
  (40 other events, 213.8 us)
where the time goes:
time: 451 us; the launch traced here: 445 us
  blocking collectives  157 us (35%)
  starting transfers between devices  124 us (27%)
  local copies, waits for them, and re-layouts  68.1 us (15%)
  waiting for transfers between devices  40.6 us (9%)
  matrix products  27 us (6%)
  other arithmetic  25 us (6%)
    all_gather x15, blocking collectives, gather_in_order(): blocks = lax.all_gather(blocks, axes[k])  157 us
    ppermute x24, starting transfers between devices, with_halo(): lax.ppermute(initial, axis, [(b, a) for a, b in up])  72.7 us
    ppermute x24, starting transfers between devices, with_halo(): lax.ppermute(last, axis, up)  29.7 us
    dot_general x80, matrix products, along_axis(): jnp.tensordot(matrix, values, axes=([1], [dimension]), precision=PRECISE)  27 us
    slice x18, local copies, waits for them, and re-layouts, coarsen(): values = values[:, :, 0::2] + values[:, :, 1::2]  23.3 us
    ppermute x6, starting transfers between devices, extended(): lax.ppermute(lax.slice_in_dim(block, 0, width, axis=dim), axis, backward)  16.1 us
    another operation x27, local copies, waits for them, and re-layouts, refine_axis(): stacked = jnp.stack([even_cells, odd_cells], axis=dimension + 1)  15.7 us
    ppermute x24, waiting for transfers between devices, with_halo(): lax.ppermute(last, axis, up)  15 us
  transfers between devices with their start and end apart: 60, of which 24 were waited for; matrix products, arithmetic and copies ran while one was open for 1% of the time, Pallas kernels for 0%

commit v1 on v0

v1 whole, which is shorter than its diff:
```python
import functools
import math

import jax
import jax.numpy as jnp
import ml_dtypes
import numpy as np
from jax import lax
from jax.experimental import pallas as pl
from jax.experimental.pallas import tpu as pltpu
from jax.sharding import PartitionSpec as P

MESH = pl.DeviceIdType.MESH
DAMPING = 6.0 / 7.0
LINEAR = ({-1: 0.25, 0: 0.75}, {0: 0.75, 1: 0.25})
CUBIC = (
    {-2: -5.0 / 128, -1: 35.0 / 128, 0: 105.0 / 128, 1: -7.0 / 128},
    {-1: -7.0 / 128, 0: 105.0 / 128, 1: 35.0 / 128, 2: -5.0 / 128},
)
GX, GY, GZ = 8, 4, 8
N_GATHER = 7 + 15 + 16
N_SEMS = 3 * N_GATHER + 4 + 24


(RZ1, RZ2, RH, QZ21, PZ21, QZ10M, QZ10H, PZ10M, PZ10H, WZ, WZL, WQ, WQL, WP, WPL) = range(15)


def fourier(n):
    j = np.arange(n)
    rows, eig = [np.full(n, math.sqrt(1.0 / n))], [0.0]
    for k in range(1, n // 2):
        for f in (np.cos, np.sin):
            rows.append(math.sqrt(2.0 / n) * f(2 * np.pi * ((k * j) % n) / n))
            eig.append(2 - 2 * np.cos(2 * np.pi * k / n))
    rows.append(math.sqrt(1.0 / n) * np.where(j % 2, -1.0, 1.0))
    eig.append(4.0)
    return np.array(rows), np.array(eig)


def halves(m):
    high = m.astype(ml_dtypes.bfloat16)
    return high, (m - high.astype(np.float64)).astype(ml_dtypes.bfloat16)


def tables():
    m = np.zeros((15, 128, 128))
    for i in range(64):
        for p in range(2):
            m[RZ1, 2 * i + p, 8 + i] = 0.125
    for i in range(32):
        for p in range(2):
            m[RZ2, 8 + 2 * i + p, i::32] = 0.125
    for k in range(4):
        for p in range(2):
            m[RH, 2 * k + p, 72 + k] = 0.125
            m[RH, 120 + 2 * k + p, 4 + k] = 0.125
    for z in range(-8, 72):
        i, p = divmod(z, 2)
        for t, w in ((QZ21, CUBIC[p]), (PZ21, LINEAR[p])):
            for off, weight in w.items():
                m[t, (32 + i + off) % 128, 8 + z] += weight
    for z in range(-8, 136):
        i, p = divmod(z, 2)
        own = 0 <= z < 128
        for t, w in ((QZ10M if own else QZ10H, CUBIC[p]), (PZ10M if own else PZ10H, LINEAR[p])):
            for off, weight in w.items():
                m[t, 8 + i + off, z % 128] += weight
    hz, ez = fourier(64)
    down = np.zeros((128, 64))
    for z in range(128):
        down[z, z // 2] = 0.125
    m[WZ, :, :64] = down @ hz.T
    for t, weights in ((WQ, CUBIC), (WP, LINEAR)):
        up = np.zeros((64, 128))
        for z in range(128):
            i, p = divmod(z, 2)
            for off, weight in weights[p].items():
                up[(i + off) % 64, z] += weight
        m[t, :64, :] = hz @ up
    mats = m.astype(ml_dtypes.bfloat16)
    for t in (WZ, WQ, WP):
        mats[t], mats[t + 1] = halves(m[t])
    h, e = fourier(16)
    hxy = np.zeros((256, 256))
    for r in range(256):
        jp, x, g = r // 128, (r // 8) % 16, r % 8
        hxy[:, r] = np.kron(h[:, x], h[:, 2 * g + jp])
    both = np.stack([*halves(hxy), *halves(hxy.T)])
    lam = np.ones((256, 128))
    lam[:, :64] = 0.25**3 * ((e[:, None] + e[None, :]).reshape(256, 1) + ez[None, :])
    return mats, both, lam.astype(np.float32)


def dot(a, b):
    return jnp.dot(a, b, preferred_element_type=jnp.float32)


def split(x):
    high = x.astype(jnp.bfloat16)
    return high, (x - high.astype(jnp.float32)).astype(jnp.bfloat16)


def mm2(x, w):
    high, low = split(x)
    return dot(high, w) + dot(low, w)


def mm3(x, w, w_low):
    high, low = split(x)
    return dot(high, w) + dot(low, w) + dot(high, w_low)


def left3(w, w_low, x):
    high, low = split(x)
    return dot(w, high) + dot(w, low) + dot(w_low, high)


def roll(x, shift, axis):
    shift %= x.shape[axis]
    return x if shift == 0 else pltpu.roll(x, shift, axis)


def weighted(weights, at):
    total = None
    for off, weight in weights.items():
        term = weight * at(off)
        total = term if total is None else total + term
    return total


def loop(start, stop, body):
    def step(i, carry):
        body(i)
        return carry

    lax.fori_loop(start, stop, step, 0)


def lanes(shape):
    return lax.broadcasted_iota(jnp.int32, shape, len(shape) - 1)


def kernel(
    shift_ref, src, mats_hbm, hxy_hbm, lam_hbm, out,
    mats, hxy, lam, A, W, f1o, LR1, LR0, H0, F1, F0M, F0H,
    G2, U2, V2, T3, TZ2, B1, V1, U1, T1, tmp, TZM, TZH, BM, BH, VM, VH, TM, TH, RM, RHH, R1, D1, E1,
    csem, ss, rs,
):
    gx, gy, gz = lax.axis_index("gx"), lax.axis_index("gy"), lax.axis_index("gz")
    core = lax.rem(gy, 2)

    def peer(dx, dy, dz):
        return (lax.rem(gx + dx % GX, GX), lax.rem(gy + dy % GY, GY), lax.rem(gz + dz % GZ, GZ))

    partner = (gx, gy + 1 - 2 * core, gz)

    loads = [
        pltpu.make_async_copy(mats_hbm, mats, csem.at[0]),
        pltpu.make_async_copy(hxy_hbm, hxy, csem.at[1]),
        pltpu.make_async_copy(lam_hbm, lam, csem.at[2]),
    ]
    for load in loads:
        load.start()

    barrier = pltpu.get_barrier_semaphore()
    friends = [(d, 0, 0) for d in range(1, 8)]
    friends += [(0, a, b) for a in (0, 2) for b in range(8) if (a, b) != (0, 0)]
    friends += [(0, 1, 0), (0, 3, 0)]
    friends += [(a, 0, b) for a in (1, 7) for b in (1, 7)]
    for f in friends:
        pl.semaphore_signal(barrier, inc=1, device_id=peer(*f), device_id_type=MESH)

    used = [0]

    def remote(source, target, device):
        k = used[0]
        used[0] += 1
        return pltpu.make_async_remote_copy(
            src_ref=source, dst_ref=target, send_sem=ss.at[k], recv_sem=rs.at[k],
            device_id=device, device_id_type=MESH,
        )

    shift = shift_ref[0]
    w = [0.25**k for k in range(4)]
    d = [6.0 * w[k] + shift for k in range(3)]
    c = [jnp.max(DAMPING / jnp.full((8, 128), d[k], jnp.float32)) for k in range(3)]

    def wrap(u):
        for j in range(4):
            u[j, 0] = u[j, 32]
            u[j, 33] = u[j, 1]

    def beside2(u, i, n):
        mid = [u[j, pl.ds(i + 1, n)] for j in range(4)]
        sums = []
        for j in range(4):
            s = u[j, pl.ds(i + 2, n)] + u[j, pl.ds(i, n)]
            s = s + (mid[j + 1] if j < 3 else roll(mid[0], -1, 1))
            s = s + (mid[j - 1] if j > 0 else roll(mid[3], 1, 1))
            s = s + roll(mid[j], -1, 2) + roll(mid[j], 1, 2)
            sums.append(s)
        return mid, sums

    def sweep2(u, v):
        def body(t):
            i = 4 * t
            mid, sums = beside2(u, i, 4)
            for j in range(4):
                g = G2[j, pl.ds(i, 4)]
                v[j, pl.ds(i + 1, 4)] = mid[j] + c[2] * (g - (d[2] * mid[j] - w[2] * sums[j]))

        loop(0, 8, body)
        wrap(v)

    def keep3(values, t):
        for jp in range(2):
            s = values[2 * jp] + values[2 * jp + 1]
            T3[jp, 2 * t] = s[0] + s[1]
            T3[jp, 2 * t + 1] = s[2] + s[3]

    def defect2(v):
        def body(t):
            i = 4 * t
            mid, sums = beside2(v, i, 4)
            keep3([G2[j, pl.ds(i, 4)] - (d[2] * mid[j] - w[2] * sums[j]) for j in range(4)], t)

        loop(0, 8, body)

    def solve3(t, weights):
        x = T3[...].reshape(256, 128)
        x = mm3(x, mats[WZ], mats[WZL])
        x = left3(hxy[0], hxy[1], x)
        x = x / (lam[...] + shift)
        x = left3(hxy[2], hxy[3], x)
        x = mm3(x, mats[t], mats[t + 1]).reshape(2, 16, 8, 128)
        result = []
        for j in range(4):
            jp, p = divmod(j, 2)

            def y_at(off):
                s, k = divmod(jp + off, 2)
                return roll(x[k], -s, 1)

            rows = weighted(weights[p], y_at)

            def x_at(off):
                return jnp.concatenate([rows[off % 16 :], rows[: off % 16]], axis=0) if off else rows

            pair = [weighted(weights[q], x_at) for q in range(2)]
            result.append(jnp.stack(pair, axis=1).reshape(32, 8, 128))
        return result

    def correct2():
        e = solve3(WP, LINEAR)
        for j in range(4):
            V2[j, 1:33] = V2[j, 1:33] + e[j]
        wrap(V2)
        sweep2(V2, U2)

    def cycle2_zero():
        def body(t):
            for j in range(4):
                V2[j, pl.ds(4 * t + 1, 4)] = c[2] * G2[j, pl.ds(4 * t, 4)]

        loop(0, 8, body)
        wrap(V2)
        defect2(V2)
        correct2()

    def restrict12(source, row):
        for x in range(4):
            s = None
            for a in range(2):
                for b in range(2):
                    part = source[2 * x + a, pl.ds(row + b, 4, stride=2), :]
                    s = part if s is None else s + part
            tmp[4 * x : 4 * x + 4] = s
        z = mm2(tmp[...], mats[RZ2])
        row_of = lax.broadcasted_iota(jnp.int32, (16, 128), 0)
        z = jnp.where(lax.div(lanes((16, 128)), 32) == lax.rem(row_of, 4), z, 0.0)
        z = z + roll(z, -1, 0)
        tmp[...] = z + roll(z, -2, 0)

    def gather_first(k):
        A[k, 8:12] = tmp[pl.ds(0, 4, stride=4), :]
        copies = []
        for dx in (4, 3, 5, 2, 6, 1, 7):
            slot = (2 - dx) % 8
            copies.append(remote(A.at[k, pl.ds(8, 4)], A.at[k, pl.ds(4 * slot, 4)], peer(dx, 0, 0)))
        for copy in copies:
            copy.start()
        return copies

    far = {0: 0, 1: 1, 2: 1, 3: 2, 4: 2, 5: 2, 6: 1, 7: 1}
    order = [(a, b) for a in (0, 2) for b in range(8) if (a, b) != (0, 0)]

    def gather_second(k, first):
        for copy in first:
            copy.wait_recv()
        W[k, 1, 32:64] = A[k]
        copies = {}
        for a, b in order:
            copies[a, b] = remote(
                A.at[k], W.at[k, (1 - a) % 4, pl.ds(32 * ((1 - b) % 8), 32)], peer(0, a, b)
            )
        for a, b in sorted(order, key=lambda o: -far[o[1]]):
            copies[a, b].start()
        return copies

    def gather_third(k, second):
        relays = []

        def relay(a, b):
            g, s = (1 - a) % 4, pl.ds(32 * ((1 - b) % 8), 32)
            to = lax.rem(g + 3 + 2 * core, 4)
            relays.append(remote(W.at[k, g, s], W.at[k, to, s], partner))
            relays[-1].start()

        relay(0, 0)
        for a, b in sorted(order, key=lambda o: far[o[1]]):
            second[a, b].wait_recv()
            relay(a, b)
        for copy in relays:
            copy.wait_recv()
        return relays

    def unpack(k):
        group = lax.div(lanes((8, 128)), 32)

        def body(x):
            blocks = [W[k, g, pl.ds(x, 8, stride=32), :] for g in range(4)]
            for j in range(4):
                total = roll(blocks[0], -32 * j, 1)
                for g in range(1, 4):
                    total = jnp.where(group == g, roll(blocks[g], 32 * (g - j), 1), total)
                G2[j, x] = total

        loop(0, 32, body)

    def refine21(table, weights):
        x = U2[:, 3:19].reshape(512, 128)
        TZ2[...] = mm2(x, mats[table]).reshape(4, 16, 8, 128)

        def body(t):
            for p in range(2):
                planes = [weighted(weights[p], lambda off: TZ2[j, t + 2 + off]) for j in range(4)]
                for j in range(4):
                    for q in range(2):

                        def y_at(off):
                            s, k = divmod(j + off, 4)
                            return roll(planes[k], -s, 0)

                        B1[2 * t + p, pl.ds(2 * j + q, 8, stride=8), :] = weighted(weights[q], y_at)

        loop(0, 12, body)

    def beside1(get, i):
        mid = get(i)
        s = get(i + 1) + get(i - 1)
        s = s + roll(mid, -1, 0) + roll(mid, 1, 0)
        s = s + roll(mid, -1, 1) + roll(mid, 1, 1)
        return mid, s

    def defect_of(mid, s, f, k):
        return f - (d[k] * mid - w[k] * s)

    def beside0(i):
        lane = lanes((32, 128))
        mid = [VM[i], VH[i]]
        up = [roll(m, -1, 1) for m in mid]
        down = [roll(m, 1, 1) for m in mid]
        sums = []
        for k, ref in enumerate((VM, VH)):
            s = ref[i + 1] + ref[i - 1]
            s = s + roll(mid[k], -1, 0) + roll(mid[k], 1, 0)
            s = s + jnp.where(lane == 127, up[1 - k], up[k]) + jnp.where(lane == 0, down[1 - k], down[k])
            sums.append(s)
        return mid, sums

    loads[0].wait()
    rows = []
    for x in range(8):
        s = None
        for a in range(2):
            for b in range(2):
                part = src[2 * x + a, pl.ds(b, 8, stride=2), :]
                s = part if s is None else s + part
        rows.append(s)
    f1o[...] = mm2(jnp.concatenate(rows, axis=0), mats[RZ1]).reshape(8, 8, 128)
    restrict12(f1o, 0)
    pl.semaphore_wait(barrier, len(friends))
    pending = []
    first = gather_first(0)
    pending += first
    side = []
    for dy, k in ((1, 0), (3, 1)):
        side.append(remote(f1o, LR1.at[k], peer(0, dy, 0)))
    for dy, k in ((1, 0), (3, 1)):
        side.append(remote(src, LR0.at[k], peer(0, dy, 0)))
    for copy in side:
        copy.start()
    pending += side

    second = gather_second(0, first)
    pending += second.values()

    side[0].wait_recv()
    side[1].wait_recv()
    lane = lanes((8, 8, 128))
    F1[8:16, 8:16] = jnp.where(
        lane < 8,
        roll(LR1[0], 64, 2),
        jnp.where(lane < 72, f1o[...], jnp.where(lane < 80, roll(LR1[1], 64, 2), 0.0)),
    )
    corner1 = []
    around = [(1, 0), (-1, 0), (0, 1), (0, -1), (1, 1), (1, -1), (-1, 1), (-1, -1)]
    for dx, dz in around:
        corner1.append(
            remote(
                F1.at[pl.ds(8, 8), pl.ds(8, 8)],
                F1.at[pl.ds(8 - 8 * dx, 8), pl.ds(8 - 8 * dz, 8)],
                peer(dx, 0, dz),
            )
        )
    for copy in corner1:
        copy.start()
    pending += corner1

    side[2].wait_recv()
    side[3].wait_recv()

    def halo0(i):
        lane = lanes((16, 128))
        H0[i] = jnp.where(lane < 8, LR0[1, i], jnp.where(lane >= 120, LR0[0, i], 0.0))
        F0M[i + 6, 8:24] = src[i]
        F0H[i + 6, 8:24] = H0[i]

    loop(0, 16, halo0)

    third = gather_third(0, second)
    pending += third

    corner0 = []
    for dx, dz in around:
        n_x, from_x, to_x = {0: (16, 0, 6), 1: (6, 10, 0), -1: (6, 0, 22)}[dx]
        n_y, from_y, to_y = {0: (16, 0, 8), 1: (8, 8, 0), -1: (8, 0, 24)}[dz]
        for source, target in ((src, F0M), (H0, F0H)):
            corner0.append(
                remote(
                    source.at[pl.ds(from_x, n_x), pl.ds(from_y, n_y)],
                    target.at[pl.ds(to_x, n_x), pl.ds(to_y, n_y)],
                    peer(dx, 0, dz),
                )
            )
    for copy in corner0:
        copy.start()
    pending += corner0

    unpack(0)
    loads[1].wait()
    loads[2].wait()

    def sum3(t):
        keep3([G2[j, pl.ds(4 * t, 4)] for j in range(4)], t)

    loop(0, 8, sum3)
    u = solve3(WQ, CUBIC)
    for j in range(4):
        U2[j, 1:33] = u[j]
    wrap(U2)
    sweep2(U2, V2)
    defect2(V2)
    correct2()

    refine21(QZ21, CUBIC)
    for copy in corner1:
        copy.wait_recv()

    def pre1(i):
        mid, s = beside1(lambda k: B1[k, 0:24], i)
        V1[i] = mid + c[1] * defect_of(mid, s, F1[i], 1)

    loop(1, 23, pre1)

    def res1(i):
        mid, s = beside1(lambda k: V1[k], i)
        T1[i - 8] = defect_of(mid, s, F1[i], 1)

    loop(8, 16, res1)
    restrict12(T1, 8)
    first = gather_first(1)
    second = gather_second(1, first)
    third = gather_third(1, second)
    pending += first + list(second.values()) + third
    unpack(1)
    cycle2_zero()
    refine21(PZ21, LINEAR)

    def add1(i):
        V1[i] = V1[i] + B1[i, 0:24]

    loop(2, 22, add1)

    def post1(i):
        mid, s = beside1(lambda k: V1[k], i)
        U1[i - 3] = mid + c[1] * defect_of(mid, s, F1[i], 1)

    loop(3, 21, post1)

    u = U1[...].reshape(432, 128)
    TZM[...] = mm2(u, mats[QZ10M]).reshape(18, 24, 128)
    TZH[...] = mm2(u, mats[QZ10H]).reshape(18, 24, 128)

    def cubic0(t):
        for source, target in ((TZM, BM), (TZH, BH)):
            for p in range(2):
                plane = weighted(CUBIC[p], lambda off: source[t + 2 + off])
                at = {off: roll(plane, -(4 + off), 0)[0:16] for off in range(-2, 3)}
                for q in range(2):
                    target[2 * t + p, pl.ds(q, 16, stride=2), :] = weighted(CUBIC[q], at.__getitem__)

    loop(0, 14, cubic0)
    for copy in corner0:
        copy.wait_recv()

    def pre0(i):
        lane = lanes((32, 128))
        refs = (BM, BH)
        mid = [ref[i] for ref in refs]
        up = [roll(m, -1, 1) for m in mid]
        down = [roll(m, 1, 1) for m in mid]
        for k, (f, v) in enumerate(((F0M, VM), (F0H, VH))):
            s = refs[k][i + 1] + refs[k][i - 1]
            s = s + roll(mid[k], -1, 0) + roll(mid[k], 1, 0)
            s = s + jnp.where(lane == 127, up[1 - k], up[k]) + jnp.where(lane == 0, down[1 - k], down[k])
            v[i] = mid[k] + c[0] * defect_of(mid[k], s, f[i], 0)

    loop(1, 27, pre0)

    def res0(t):
        for a in range(2):
            i = 2 * t + 2 + a
            mid, sums = beside0(i)
            for k, (f, target) in enumerate(((F0M, TM), (F0H, TH))):
                r = defect_of(mid[k], sums[k], f[i], 0)
                target[t] = r if a == 0 else target[t] + r
        for source, target in ((TM, RM), (TH, RHH)):
            target[t] = source[t, pl.ds(0, 16, stride=2), :] + source[t, pl.ds(1, 16, stride=2), :]

    loop(0, 12, res0)
    R1[...] = (
        mm2(RM[...].reshape(192, 128), mats[RZ1]) + mm2(RHH[...].reshape(192, 128), mats[RH])
    ).reshape(12, 16, 128)

    def zero1(i):
        D1[i] = c[1] * R1[i]

    loop(0, 12, zero1)

    def res1b(i):
        mid, s = beside1(lambda k: D1[k], i)
        T1[i - 2, 0:16] = defect_of(mid, s, R1[i], 1)

    loop(2, 10, res1b)
    restrict12(T1, 4)
    first = gather_first(2)
    second = gather_second(2, first)
    third = gather_third(2, second)
    pending += first + list(second.values()) + third
    unpack(2)
    cycle2_zero()
    refine21(PZ21, LINEAR)

    def add1b(i):
        D1[i] = D1[i] + B1[i + 6, 4:20]

    loop(0, 12, add1b)
    E1[0] = jnp.zeros((16, 128), jnp.float32)
    E1[11] = jnp.zeros((16, 128), jnp.float32)

    def post1b(i):
        mid, s = beside1(lambda k: D1[k], i)
        E1[i] = mid + c[1] * defect_of(mid, s, R1[i], 1)

    loop(1, 11, post1b)

    e = E1[...].reshape(192, 128)
    TZM[0:12, 0:16] = mm2(e, mats[PZ10M]).reshape(12, 16, 128)
    TZH[0:12, 0:16] = mm2(e, mats[PZ10H]).reshape(12, 16, 128)

    def linear0(t):
        for source, target, v in ((TZM, BM, VM), (TZH, BH, VH)):
            for p in range(2):
                plane = weighted(LINEAR[p], lambda off: source[t + 1 + off, 0:16])
                i = 2 * t + 4 + p
                for q in range(2):
                    target[i, pl.ds(q, 16, stride=2), :] = weighted(LINEAR[q], lambda off: roll(plane, -off, 0))
                v[i] = v[i] + target[i]

    loop(0, 10, linear0)

    def post0(i):
        mid, sums = beside0(i)
        v = mid[0] + c[0] * defect_of(mid[0], sums[0], F0M[i], 0)
        out[i - 6] = v[8:24]

    loop(6, 22, post0)
    for copy in pending:
        copy.wait_send()


def solution(mesh):
    mats, hxy, lam = tables()
    f32 = jnp.float32
    vmem = pltpu.VMEM
    scratch = [
        vmem((15, 128, 128), jnp.bfloat16),
        vmem((4, 256, 256), jnp.bfloat16),
        vmem((256, 128), f32),
        vmem((3, 32, 128), f32),
        vmem((3, 4, 256, 128), f32),
        vmem((8, 8, 128), f32),
        vmem((2, 8, 8, 128), f32),
        vmem((2, 16, 16, 128), f32),
        vmem((16, 16, 128), f32),
        vmem((24, 24, 128), f32),
        vmem((28, 32, 128), f32),
        vmem((28, 32, 128), f32),
        vmem((4, 32, 8, 128), f32),
        vmem((4, 34, 8, 128), f32),
        vmem((4, 34, 8, 128), f32),
        vmem((2, 16, 8, 128), f32),
        vmem((4, 16, 8, 128), f32),
        vmem((24, 64, 128), f32),
        vmem((24, 24, 128), f32),
        vmem((18, 24, 128), f32),
        vmem((8, 24, 128), f32),
        vmem((16, 128), f32),
        vmem((18, 24, 128), f32),
        vmem((18, 24, 128), f32),
        vmem((28, 32, 128), f32),
        vmem((28, 32, 128), f32),
        vmem((28, 32, 128), f32),
        vmem((28, 32, 128), f32),
        vmem((12, 32, 128), f32),
        vmem((12, 32, 128), f32),
        vmem((12, 16, 128), f32),
        vmem((12, 16, 128), f32),
        vmem((12, 16, 128), f32),
        vmem((12, 16, 128), f32),
        vmem((12, 16, 128), f32),
        pltpu.SemaphoreType.DMA((3,)),
        pltpu.SemaphoreType.DMA((N_SEMS,)),
        pltpu.SemaphoreType.DMA((N_SEMS,)),
    ]

    def step(source, shift):
        return pl.pallas_call(
            kernel,
            out_shape=jax.ShapeDtypeStruct(source.shape, f32),
            in_specs=[
                pl.BlockSpec(memory_space=pltpu.SMEM),
                pl.BlockSpec(memory_space=vmem),
                pl.BlockSpec(memory_space=pl.ANY),
                pl.BlockSpec(memory_space=pl.ANY),
                pl.BlockSpec(memory_space=pl.ANY),
            ],
            out_specs=pl.BlockSpec(memory_space=vmem),
            scratch_shapes=scratch,
            compiler_params=pltpu.CompilerParams(collective_id=0, has_side_effects=True),
            name="fcycle",
        )(shift, source, jnp.asarray(mats), jnp.asarray(hxy), jnp.asarray(lam))

    spec = P("gx", "gz", "gy")
    return jax.shard_map(step, mesh=mesh, in_specs=(spec, P()), out_specs=spec, check_vma=False)
```

time: 451 us -> 87.5 us (0.19); the launches traced: 445 us -> 87.3 us
  blocking collectives: 157 us -> 0 us
  starting transfers between devices: 124 us -> 0 us
  Pallas kernels: 0 us -> 85.1 us
  local copies, waits for them, and re-layouts: 68.1 us -> 1.57 us
  waiting for transfers between devices: 40.6 us -> 0 us
  matrix products: 27 us -> 0 us
  other arithmetic: 25 us -> 0 us
    all_gather x15 -> x0, blocking collectives: 157 us -> none  [gather_in_order(): blocks = lax.all_gather(blocks, axes[k])]
    ppermute x60 -> x0, starting transfers between devices: 124 us -> none  [the longest x24 72.7 us: with_halo(): lax.ppermute(initial, axis, [(b, a) for a, b in up])]
    pallas_call x0 -> x1, Pallas kernels: none -> 85.1 us  [step(): pl.pallas_call(kernel, out_shape=jax.ShapeDtypeStruct(source.shape, f32),...]
    ppermute x60 -> x0, waiting for transfers between devices: 40.6 us -> none  [the longest x24 15 us: with_halo(): lax.ppermute(last, axis, up)]
    slice x102 -> x0, local copies, waits for them, and re-layouts: 31.4 us -> none  [the longest x18 23.3 us: coarsen(): values = values[:, :, 0::2] + values[:, :, 1::2]]
    dot_general x80 -> x0, matrix products: 27 us -> none  [along_axis(): jnp.tensordot(matrix, values, axes=([1], [dimension]), precision=PRECISE)]
    another operation x27 -> x0, local copies, waits for them, and re-layouts: 15.7 us -> none  [refine_axis(): stacked = jnp.stack([even_cells, odd_cells], axis=dimension + 1)]
    reshape x12 -> x0, local copies, waits for them, and re-layouts: 10.6 us -> none  [the longest x9 7.93 us: refine_axis(): return stacked.reshape(new_shape)]
  transfers between devices with their start and end apart: 60 -> 0, of which waited for: 24 -> 0; matrix products, arithmetic and copies ran while one was open for 1% -> 0% of each run, Pallas kernels for 0% -> 0%
where the time goes in v1:
time: 87.5 us; the launch traced here: 87.3 us
  Pallas kernels  85.1 us (97%)
  local copies, waits for them, and re-layouts  1.57 us (2%)
    pallas_call x1, Pallas kernels, step(): pl.pallas_call(kernel, out_shape=jax.ShapeDtypeStruct(source.shape, f32),...  85.1 us

profile of v1, /device:TPU:1, one launch (start us, length us, event | category | flops | bytes accessed | tf_op | source)
XLA Modules:
  0.0 87.3 jit_solution(2831494518099005655)
XLA Ops:
  0.7 85.1 %fcycle.1 = f32[16,16,128]{2,1,0:T(8,128)} custom-call(f32[1]{0:T(128)S(6)} %copy.7.shift_ref, f32[16,16,128]{2,1,0:T(8,128)} %src.1, bf16[15,128,128]{2,1,0:T(8,128)(2,1)} %constant.6.clone.mats_hbm, bf16[4,256,256]{2,1,0:T(8,128)(2,1)} %constant.7.clone.hxy_hbm, f32[256,128]{1,0:T(8,128)} %constant.8.clone.lam_hbm), custom_call_target="tpu_custom_call" | custom-call | tf_op jit(solution)/shard_map/fcycle/pallas_call | solution.py:659
  85.8 1.6 %copy.8 = f32[16,16,128]{2,1,0:T(8,128)} copy(f32[16,16,128]{2,1,0:T(8,128)} %fcycle.1) | data formatting | bytes 262144

commit v2 on v1

--- a/solution.py
+++ b/solution.py
@@ -20,6 +20,7 @@
 GX, GY, GZ = 8, 4, 8
 N_GATHER = 7 + 15 + 16
 N_SEMS = 3 * N_GATHER + 4 + 24
+SLOT = 33
 
 
 (RZ1, RZ2, RH, QZ21, PZ21, QZ10M, QZ10H, PZ10M, PZ10H, WZ, WZL, WQ, WQL, WP, WPL) = range(15)
@@ -128,12 +129,19 @@
     return total
 
 
-def loop(start, stop, body):
+def loop(start, stop, body, unroll=1):
+    trips = (stop - start) // unroll
+    assert trips * unroll == stop - start
+
     def step(i, carry):
-        body(i)
+        for k in range(unroll):
+            body(start + i * unroll + k)
         return carry
 
-    lax.fori_loop(start, stop, step, 0)
+    if trips == 1:
+        step(0, 0)
+    else:
+        lax.fori_loop(0, trips, step, 0)
 
 
 def lanes(shape):
@@ -141,8 +149,8 @@
 
 
 def kernel(
-    shift_ref, src, mats_hbm, hxy_hbm, lam_hbm, out,
-    mats, hxy, lam, A, W, f1o, LR1, LR0, H0, F1, F0M, F0H,
+    shift_hbm, src_hbm, mats_hbm, hxy_hbm, lam_hbm, out,
+    shift_ref, src, mats, hxy, lam, A, W, f1o, LR1, LR0, H0, F1, F0M, F0H,
     G2, U2, V2, T3, TZ2, B1, V1, U1, T1, tmp, TZM, TZH, BM, BH, VM, VH, TM, TH, RM, RHH, R1, D1, E1,
     csem, ss, rs,
 ):
@@ -153,14 +161,6 @@
         return (lax.rem(gx + dx % GX, GX), lax.rem(gy + dy % GY, GY), lax.rem(gz + dz % GZ, GZ))
 
     partner = (gx, gy + 1 - 2 * core, gz)
-
-    loads = [
-        pltpu.make_async_copy(mats_hbm, mats, csem.at[0]),
-        pltpu.make_async_copy(hxy_hbm, hxy, csem.at[1]),
-        pltpu.make_async_copy(lam_hbm, lam, csem.at[2]),
-    ]
-    for load in loads:
-        load.start()
 
     barrier = pltpu.get_barrier_semaphore()
     friends = [(d, 0, 0) for d in range(1, 8)]
@@ -170,6 +170,18 @@
     for f in friends:
         pl.semaphore_signal(barrier, inc=1, device_id=peer(*f), device_id_type=MESH)
 
+    inputs = [
+        pltpu.make_async_copy(src_hbm, src, csem.at[3]),
+        pltpu.make_async_copy(shift_hbm, shift_ref, csem.at[4]),
+    ]
+    loads = [
+        pltpu.make_async_copy(mats_hbm, mats, csem.at[0]),
+        pltpu.make_async_copy(hxy_hbm, hxy, csem.at[1]),
+        pltpu.make_async_copy(lam_hbm, lam, csem.at[2]),
+    ]
+    for load in inputs + loads:
+        load.start()
+
     used = [0]
 
     def remote(source, target, device):
@@ -179,11 +191,6 @@
             src_ref=source, dst_ref=target, send_sem=ss.at[k], recv_sem=rs.at[k],
             device_id=device, device_id_type=MESH,
         )
-
-    shift = shift_ref[0]
-    w = [0.25**k for k in range(4)]
-    d = [6.0 * w[k] + shift for k in range(3)]
-    c = [jnp.max(DAMPING / jnp.full((8, 128), d[k], jnp.float32)) for k in range(3)]
 
     def wrap(u):
         for j in range(4):
@@ -201,16 +208,15 @@
             sums.append(s)
         return mid, sums
 
-    def sweep2(u, v):
+    def sweep2(u, v, start, stop):
         def body(t):
-            i = 4 * t
+            i = 4 * t + start
             mid, sums = beside2(u, i, 4)
             for j in range(4):
-                g = G2[j, pl.ds(i, 4)]
+                g = G2[j, pl.ds(i + 1, 4)]
                 v[j, pl.ds(i + 1, 4)] = mid[j] + c[2] * (g - (d[2] * mid[j] - w[2] * sums[j]))
 
-        loop(0, 8, body)
-        wrap(v)
+        loop(0, (stop - start) // 4, body, 4)
 
     def keep3(values, t):
         for jp in range(2):
@@ -218,15 +224,22 @@
             T3[jp, 2 * t] = s[0] + s[1]
             T3[jp, 2 * t + 1] = s[2] + s[3]
 
-    def defect2(v):
+    def defect2():
         def body(t):
             i = 4 * t
-            mid, sums = beside2(v, i, 4)
-            keep3([G2[j, pl.ds(i, 4)] - (d[2] * mid[j] - w[2] * sums[j]) for j in range(4)], t)
-
-        loop(0, 8, body)
-
-    def solve3(t, weights):
+            mid, sums = beside2(V2, i, 4)
+            keep3([G2[j, pl.ds(i + 1, 4)] - (d[2] * mid[j] - w[2] * sums[j]) for j in range(4)], t)
+
+        loop(0, 8, body, 4)
+
+    def defect2_zero():
+        def body(t):
+            mid, sums = beside2(G2, 4 * t, 4)
+            keep3([mid[j] - c[2] * (d[2] * mid[j] - w[2] * sums[j]) for j in range(4)], t)
+
+        loop(0, 8, body, 4)
+
+    def solve3(t, weights, start, stop):
         x = T3[...].reshape(256, 128)
         x = mm3(x, mats[WZ], mats[WZL])
         x = left3(hxy[0], hxy[1], x)
@@ -244,28 +257,30 @@
             rows = weighted(weights[p], y_at)
 
             def x_at(off):
-                return jnp.concatenate([rows[off % 16 :], rows[: off % 16]], axis=0) if off else rows
+                low, high = start // 2 + off, stop // 2 + off
+                parts = [rows[max(low, 0) : min(high, 16)]]
+                if low < 0:
+                    parts.insert(0, rows[low % 16 :])
+                if high > 16:
+                    parts.append(rows[: high - 16])
+                return parts[0] if len(parts) == 1 else jnp.concatenate(parts, axis=0)
 
             pair = [weighted(weights[q], x_at) for q in range(2)]
-            result.append(jnp.stack(pair, axis=1).reshape(32, 8, 128))
+            result.append(jnp.stack(pair, axis=1).reshape(stop - start, 8, 128))
         return result
 
-    def correct2():
-        e = solve3(WP, LINEAR)
+    def correct2(zero):
+        e = solve3(WP, LINEAR, 0, 20)
         for j in range(4):
-            V2[j, 1:33] = V2[j, 1:33] + e[j]
-        wrap(V2)
-        sweep2(V2, U2)
+            if zero:
+                V2[j, 1:21] = c[2] * G2[j, 1:21] + e[j]
+            else:
+                V2[j, 1:21] = V2[j, 1:21] + e[j]
+        sweep2(V2, U2, 2, 18)
 
     def cycle2_zero():
-        def body(t):
-            for j in range(4):
-                V2[j, pl.ds(4 * t + 1, 4)] = c[2] * G2[j, pl.ds(4 * t, 4)]
-
-        loop(0, 8, body)
-        wrap(V2)
-        defect2(V2)
-        correct2()
+        defect2_zero()
+        correct2(True)
 
     def restrict12(source, row):
         for x in range(4):
@@ -297,11 +312,11 @@
     def gather_second(k, first):
         for copy in first:
             copy.wait_recv()
-        W[k, 1, 32:64] = A[k]
+        W[k, 1, SLOT : SLOT + 32] = A[k]
         copies = {}
         for a, b in order:
             copies[a, b] = remote(
-                A.at[k], W.at[k, (1 - a) % 4, pl.ds(32 * ((1 - b) % 8), 32)], peer(0, a, b)
+                A.at[k], W.at[k, (1 - a) % 4, pl.ds(SLOT * ((1 - b) % 8), 32)], peer(0, a, b)
             )
         for a, b in sorted(order, key=lambda o: -far[o[1]]):
             copies[a, b].start()
@@ -311,7 +326,7 @@
         relays = []
 
         def relay(a, b):
-            g, s = (1 - a) % 4, pl.ds(32 * ((1 - b) % 8), 32)
+            g, s = (1 - a) % 4, pl.ds(SLOT * ((1 - b) % 8), 32)
             to = lax.rem(g + 3 + 2 * core, 4)
             relays.append(remote(W.at[k, g, s], W.at[k, to, s], partner))
             relays[-1].start()
@@ -328,14 +343,19 @@
         group = lax.div(lanes((8, 128)), 32)
 
         def body(x):
-            blocks = [W[k, g, pl.ds(x, 8, stride=32), :] for g in range(4)]
+            rows = [W[k, g, pl.ds(x, 8, stride=SLOT), :] for g in range(4)]
+            for far in (1, 2):
+                low = lax.rem(lax.div(group, far), 2) == 0
+                for g in range(4):
+                    if g & far == 0:
+                        first, second = rows[g], rows[g + far]
+                        rows[g] = jnp.where(low, first, roll(second, 32 * far, 1))
+                        rows[g + far] = jnp.where(low, roll(first, -32 * far, 1), second)
             for j in range(4):
-                total = roll(blocks[0], -32 * j, 1)
-                for g in range(1, 4):
-                    total = jnp.where(group == g, roll(blocks[g], 32 * (g - j), 1), total)
-                G2[j, x] = total
-
-        loop(0, 32, body)
+                G2[j, x + 1] = rows[j]
+
+        loop(0, 32, body, 16)
+        wrap(G2)
 
     def refine21(table, weights):
         x = U2[:, 3:19].reshape(512, 128)
@@ -351,9 +371,9 @@
                             s, k = divmod(j + off, 4)
                             return roll(planes[k], -s, 0)
 
-                        B1[2 * t + p, pl.ds(2 * j + q, 8, stride=8), :] = weighted(weights[q], y_at)
-
-        loop(0, 12, body)
+                        B1[2 * t + p, pl.ds(2 * j + q, 4, stride=8), :] = weighted(weights[q], y_at)[0:4]
+
+        loop(0, 12, body, 3)
 
     def beside1(get, i):
         mid = get(i)
@@ -367,17 +387,18 @@
 
     def beside0(i):
         lane = lanes((32, 128))
-        mid = [VM[i], VH[i]]
+        mid = [VM[i, 0:32], VH[i, 0:32]]
         up = [roll(m, -1, 1) for m in mid]
         down = [roll(m, 1, 1) for m in mid]
         sums = []
         for k, ref in enumerate((VM, VH)):
-            s = ref[i + 1] + ref[i - 1]
+            s = ref[i + 1, 0:32] + ref[i - 1, 0:32]
             s = s + roll(mid[k], -1, 0) + roll(mid[k], 1, 0)
             s = s + jnp.where(lane == 127, up[1 - k], up[k]) + jnp.where(lane == 0, down[1 - k], down[k])
             sums.append(s)
         return mid, sums
 
+    inputs[0].wait()
     loads[0].wait()
     rows = []
     for x in range(8):
@@ -389,6 +410,12 @@
         rows.append(s)
     f1o[...] = mm2(jnp.concatenate(rows, axis=0), mats[RZ1]).reshape(8, 8, 128)
     restrict12(f1o, 0)
+    inputs[1].wait()
+    shift = shift_ref[0]
+    w = [0.25**k for k in range(4)]
+    d = [6.0 * w[k] + shift for k in range(3)]
+    c = [jnp.max(DAMPING / jnp.full((8, 128), d[k], jnp.float32)) for k in range(3)]
+
     pl.semaphore_wait(barrier, len(friends))
     pending = []
     first = gather_first(0)
@@ -436,7 +463,7 @@
         F0M[i + 6, 8:24] = src[i]
         F0H[i + 6, 8:24] = H0[i]
 
-    loop(0, 16, halo0)
+    loop(0, 16, halo0, 2)
 
     third = gather_third(0, second)
     pending += third
@@ -462,16 +489,17 @@
     loads[2].wait()
 
     def sum3(t):
-        keep3([G2[j, pl.ds(4 * t, 4)] for j in range(4)], t)
-
-    loop(0, 8, sum3)
-    u = solve3(WQ, CUBIC)
+        keep3([G2[j, pl.ds(4 * t + 1, 4)] for j in range(4)], t)
+
+    loop(0, 8, sum3, 2)
+    u = solve3(WQ, CUBIC, 0, 32)
     for j in range(4):
         U2[j, 1:33] = u[j]
     wrap(U2)
-    sweep2(U2, V2)
-    defect2(V2)
-    correct2()
+    sweep2(U2, V2, 0, 32)
+    wrap(V2)
+    defect2()
+    correct2(False)
 
     refine21(QZ21, CUBIC)
     for copy in corner1:
@@ -481,13 +509,13 @@
         mid, s = beside1(lambda k: B1[k, 0:24], i)
         V1[i] = mid + c[1] * defect_of(mid, s, F1[i], 1)
 
-    loop(1, 23, pre1)
+    loop(1, 23, pre1, 11)
 
     def res1(i):
         mid, s = beside1(lambda k: V1[k], i)
         T1[i - 8] = defect_of(mid, s, F1[i], 1)
 
-    loop(8, 16, res1)
+    loop(8, 16, res1, 8)
     restrict12(T1, 8)
     first = gather_first(1)
     second = gather_second(1, first)
@@ -500,13 +528,13 @@
     def add1(i):
         V1[i] = V1[i] + B1[i, 0:24]
 
-    loop(2, 22, add1)
+    loop(2, 22, add1, 4)
 
     def post1(i):
         mid, s = beside1(lambda k: V1[k], i)
         U1[i - 3] = mid + c[1] * defect_of(mid, s, F1[i], 1)
 
-    loop(3, 21, post1)
+    loop(3, 21, post1, 9)
 
     u = U1[...].reshape(432, 128)
     TZM[...] = mm2(u, mats[QZ10M]).reshape(18, 24, 128)
@@ -520,49 +548,49 @@
                 for q in range(2):
                     target[2 * t + p, pl.ds(q, 16, stride=2), :] = weighted(CUBIC[q], at.__getitem__)
 
-    loop(0, 14, cubic0)
+    loop(0, 14, cubic0, 2)
     for copy in corner0:
         copy.wait_recv()
 
     def pre0(i):
         lane = lanes((32, 128))
         refs = (BM, BH)
-        mid = [ref[i] for ref in refs]
+        mid = [ref[i, 0:32] for ref in refs]
         up = [roll(m, -1, 1) for m in mid]
         down = [roll(m, 1, 1) for m in mid]
         for k, (f, v) in enumerate(((F0M, VM), (F0H, VH))):
-            s = refs[k][i + 1] + refs[k][i - 1]
+            s = refs[k][i + 1, 0:32] + refs[k][i - 1, 0:32]
             s = s + roll(mid[k], -1, 0) + roll(mid[k], 1, 0)
             s = s + jnp.where(lane == 127, up[1 - k], up[k]) + jnp.where(lane == 0, down[1 - k], down[k])
-            v[i] = mid[k] + c[0] * defect_of(mid[k], s, f[i], 0)
-
-    loop(1, 27, pre0)
+            v[i, 0:32] = mid[k] + c[0] * defect_of(mid[k], s, f[i, 0:32], 0)
+
+    loop(1, 27, pre0, 13)
 
     def res0(t):
         for a in range(2):
             i = 2 * t + 2 + a
             mid, sums = beside0(i)
             for k, (f, target) in enumerate(((F0M, TM), (F0H, TH))):
-                r = defect_of(mid[k], sums[k], f[i], 0)
-                target[t] = r if a == 0 else target[t] + r
+                r = defect_of(mid[k], sums[k], f[i, 0:32], 0)
+                target[t, 0:32] = r if a == 0 else target[t, 0:32] + r
         for source, target in ((TM, RM), (TH, RHH)):
-            target[t] = source[t, pl.ds(0, 16, stride=2), :] + source[t, pl.ds(1, 16, stride=2), :]
-
-    loop(0, 12, res0)
-    R1[...] = (
-        mm2(RM[...].reshape(192, 128), mats[RZ1]) + mm2(RHH[...].reshape(192, 128), mats[RH])
+            target[t, 0:16] = source[t, pl.ds(0, 16, stride=2), :] + source[t, pl.ds(1, 16, stride=2), :]
+
+    loop(0, 12, res0, 6)
+    R1[:, 0:16] = (
+        mm2(RM[:, 0:16].reshape(192, 128), mats[RZ1]) + mm2(RHH[:, 0:16].reshape(192, 128), mats[RH])
     ).reshape(12, 16, 128)
 
     def zero1(i):
-        D1[i] = c[1] * R1[i]
-
-    loop(0, 12, zero1)
+        D1[i, 0:16] = c[1] * R1[i, 0:16]
+
+    loop(0, 12, zero1, 4)
 
     def res1b(i):
-        mid, s = beside1(lambda k: D1[k], i)
-        T1[i - 2, 0:16] = defect_of(mid, s, R1[i], 1)
-
-    loop(2, 10, res1b)
+        mid, s = beside1(lambda k: D1[k, 0:16], i)
+        T1[i - 2, 0:16] = defect_of(mid, s, R1[i, 0:16], 1)
+
+    loop(2, 10, res1b, 8)
     restrict12(T1, 4)
     first = gather_first(2)
     second = gather_second(2, first)
@@ -573,19 +601,19 @@
     refine21(PZ21, LINEAR)
 
     def add1b(i):
-        D1[i] = D1[i] + B1[i + 6, 4:20]
-
-    loop(0, 12, add1b)
-    E1[0] = jnp.zeros((16, 128), jnp.float32)
-    E1[11] = jnp.zeros((16, 128), jnp.float32)
+        D1[i, 0:16] = D1[i, 0:16] + B1[i + 6, 4:20]
+
+    loop(0, 12, add1b, 4)
+    E1[0, 0:16] = jnp.zeros((16, 128), jnp.float32)
+    E1[11, 0:16] = jnp.zeros((16, 128), jnp.float32)
 
     def post1b(i):
-        mid, s = beside1(lambda k: D1[k], i)
-        E1[i] = mid + c[1] * defect_of(mid, s, R1[i], 1)
-
-    loop(1, 11, post1b)
-
-    e = E1[...].reshape(192, 128)
+        mid, s = beside1(lambda k: D1[k, 0:16], i)
+        E1[i, 0:16] = mid + c[1] * defect_of(mid, s, R1[i, 0:16], 1)
+
+    loop(1, 11, post1b, 10)
+
+    e = E1[:, 0:16].reshape(192, 128)
     TZM[0:12, 0:16] = mm2(e, mats[PZ10M]).reshape(12, 16, 128)
     TZH[0:12, 0:16] = mm2(e, mats[PZ10H]).reshape(12, 16, 128)
 
@@ -596,16 +624,16 @@
                 i = 2 * t + 4 + p
                 for q in range(2):
                     target[i, pl.ds(q, 16, stride=2), :] = weighted(LINEAR[q], lambda off: roll(plane, -off, 0))
-                v[i] = v[i] + target[i]
-
-    loop(0, 10, linear0)
+                v[i, 0:32] = v[i, 0:32] + target[i, 0:32]
+
+    loop(0, 10, linear0, 2)
 
     def post0(i):
         mid, sums = beside0(i)
-        v = mid[0] + c[0] * defect_of(mid[0], sums[0], F0M[i], 0)
+        v = mid[0] + c[0] * defect_of(mid[0], sums[0], F0M[i, 0:32], 0)
         out[i - 6] = v[8:24]
 
-    loop(6, 22, post0)
+    loop(6, 22, post0, 8)
     for copy in pending:
         copy.wait_send()
 
@@ -615,42 +643,44 @@
     f32 = jnp.float32
     vmem = pltpu.VMEM
     scratch = [
+        pltpu.SMEM((1,), f32),
+        vmem((16, 16, 128), f32),
         vmem((15, 128, 128), jnp.bfloat16),
         vmem((4, 256, 256), jnp.bfloat16),
         vmem((256, 128), f32),
         vmem((3, 32, 128), f32),
-        vmem((3, 4, 256, 128), f32),
+        vmem((3, 4, 8 * SLOT, 128), f32),
         vmem((8, 8, 128), f32),
         vmem((2, 8, 8, 128), f32),
         vmem((2, 16, 16, 128), f32),
         vmem((16, 16, 128), f32),
         vmem((24, 24, 128), f32),
-        vmem((28, 32, 128), f32),
-        vmem((28, 32, 128), f32),
-        vmem((4, 32, 8, 128), f32),
+        vmem((28, 40, 128), f32),
+        vmem((28, 40, 128), f32),
+        vmem((4, 34, 8, 128), f32),
         vmem((4, 34, 8, 128), f32),
         vmem((4, 34, 8, 128), f32),
         vmem((2, 16, 8, 128), f32),
         vmem((4, 16, 8, 128), f32),
-        vmem((24, 64, 128), f32),
+        vmem((24, 40, 128), f32),
         vmem((24, 24, 128), f32),
         vmem((18, 24, 128), f32),
         vmem((8, 24, 128), f32),
         vmem((16, 128), f32),
         vmem((18, 24, 128), f32),
         vmem((18, 24, 128), f32),
-        vmem((28, 32, 128), f32),
-        vmem((28, 32, 128), f32),
-        vmem((28, 32, 128), f32),
-        vmem((28, 32, 128), f32),
-        vmem((12, 32, 128), f32),
-        vmem((12, 32, 128), f32),
-        vmem((12, 16, 128), f32),
-        vmem((12, 16, 128), f32),
-        vmem((12, 16, 128), f32),
-        vmem((12, 16, 128), f32),
-        vmem((12, 16, 128), f32),
-        pltpu.SemaphoreType.DMA((3,)),
+        vmem((28, 40, 128), f32),
+        vmem((28, 40, 128), f32),
+        vmem((28, 40, 128), f32),
+        vmem((28, 40, 128), f32),
+        vmem((12, 40, 128), f32),
+        vmem((12, 40, 128), f32),
+        vmem((12, 24, 128), f32),
+        vmem((12, 24, 128), f32),
+        vmem((12, 24, 128), f32),
+        vmem((12, 24, 128), f32),
+        vmem((12, 24, 128), f32),
+        pltpu.SemaphoreType.DMA((5,)),
         pltpu.SemaphoreType.DMA((N_SEMS,)),
         pltpu.SemaphoreType.DMA((N_SEMS,)),
     ]
@@ -660,12 +690,9 @@
             kernel,
             out_shape=jax.ShapeDtypeStruct(source.shape, f32),
             in_specs=[
-                pl.BlockSpec(memory_space=pltpu.SMEM),
-                pl.BlockSpec(memory_space=vmem),
                 pl.BlockSpec(memory_space=pl.ANY),
-                pl.BlockSpec(memory_space=pl.ANY),
-                pl.BlockSpec(memory_space=pl.ANY),
-            ],
+            ]
+            * 5,
             out_specs=pl.BlockSpec(memory_space=vmem),
             scratch_shapes=scratch,
             compiler_params=pltpu.CompilerParams(collective_id=0, has_side_effects=True),

time: 87.5 us -> 67.9 us (0.78)
  Pallas kernels: 85.1 us -> 65.6 us
    pallas_call x1, Pallas kernels: 85.1 us -> 65.6 us  [step(): pl.pallas_call(kernel, out_shape=jax.ShapeDtypeStruct(source.shape, f32),...]
where the time goes in v2:
time: 67.9 us; the launch traced here: 67.8 us
  Pallas kernels  65.6 us (97%)
  local copies, waits for them, and re-layouts  1.57 us (2%)
    pallas_call x1, Pallas kernels, step(): pl.pallas_call(kernel, out_shape=jax.ShapeDtypeStruct(source.shape, f32),...  65.6 us
    unnamed x1, local copies, waits for them, and re-layouts  1.57 us

profile of v2, /device:TPU:1, one launch (start us, length us, event | category | flops | bytes accessed | tf_op | source)
XLA Modules:
  0.0 67.8 jit_solution(16772280437386128202)
XLA Ops:
  0.7 65.6 %fcycle.1 = f32[16,16,128]{2,1,0:T(8,128)} custom-call(f32[1]{0:T(128)S(6)} %copy.7.shift_hbm, f32[16,16,128]{2,1,0:T(8,128)} %src_hbm.1, bf16[15,128,128]{2,1,0:T(8,128)(2,1)} %constant.6.clone.mats_hbm, bf16[4,256,256]{2,1,0:T(8,128)(2,1)} %constant.7.clone.hxy_hbm, f32[256,128]{1,0:T(8,128)} %constant.8.clone.lam_hbm), custom_call_target="tpu_custom_call" | custom-call | tf_op jit(solution)/shard_map/fcycle/pallas_call | solution.py:689
  66.3 1.6 %copy.8 = f32[16,16,128]{2,1,0:T(8,128)} copy(f32[16,16,128]{2,1,0:T(8,128)} %fcycle.1) | data formatting | bytes 262144

commit v3 on v2

--- a/solution.py
+++ b/solution.py
@@ -18,12 +18,12 @@
     {-1: -7.0 / 128, 0: 105.0 / 128, 1: 35.0 / 128, 2: -5.0 / 128},
 )
 GX, GY, GZ = 8, 4, 8
-N_GATHER = 7 + 15 + 16
+N_GATHER = 7 + 2 * 15 + 16
 N_SEMS = 3 * N_GATHER + 4 + 24
-SLOT = 33
-
-
-(RZ1, RZ2, RH, QZ21, PZ21, QZ10M, QZ10H, PZ10M, PZ10H, WZ, WZL, WQ, WQL, WP, WPL) = range(15)
+SLOT = 40
+
+
+(RZ1, RZ2, RH, QZ21, PZ21, QZ10M, QZ10H, PZ10M, PZ10H, WZ, WZL, WQ, WQL, WP, WPL, PACK, OPEN) = range(17)
 
 
 def fourier(n):
@@ -44,7 +44,7 @@
 
 
 def tables():
-    m = np.zeros((15, 128, 128))
+    m = np.zeros((17, 128, 128))
     for i in range(64):
         for p in range(2):
             m[RZ1, 2 * i + p, 8 + i] = 0.125
@@ -66,6 +66,10 @@
         for t, w in ((QZ10M if own else QZ10H, CUBIC[p]), (PZ10M if own else PZ10H, LINEAR[p])):
             for off, weight in w.items():
                 m[t, 8 + i + off, z % 128] += weight
+    for y in range(8):
+        for t in range(16):
+            z = t if t < 8 else 112 + t
+            m[PACK, z, 16 * y + t] = m[OPEN, 16 * y + t, z] = 1.0
     hz, ez = fourier(64)
     down = np.zeros((128, 64))
     for z in range(128):
@@ -150,7 +154,7 @@
 
 def kernel(
     shift_hbm, src_hbm, mats_hbm, hxy_hbm, lam_hbm, out,
-    shift_ref, src, mats, hxy, lam, A, W, f1o, LR1, LR0, H0, F1, F0M, F0H,
+    shift_ref, src, mats, hxy, lam, A, W, f1o, LR1, LR0, PK, HP, F1, F0M, F0H,
     G2, U2, V2, T3, TZ2, B1, V1, U1, T1, tmp, TZM, TZH, BM, BH, VM, VH, TM, TH, RM, RHH, R1, D1, E1,
     csem, ss, rs,
 ):
@@ -161,6 +165,17 @@
         return (lax.rem(gx + dx % GX, GX), lax.rem(gy + dy % GY, GY), lax.rem(gz + dz % GZ, GZ))
 
     partner = (gx, gy + 1 - 2 * core, gz)
+
+    x_hi = lax.rem(gz, 2)
+    turn = 1 - 2 * x_hi
+    order = [(lo, hi, dy) for lo in range(2) for hi in range(2) for dy in range(4)]
+
+    def steps(o):
+        return ((0, 1), (2, 1))[o[1]][o[0]] + min(o[2], 4 - o[2])
+
+    order.sort(key=steps)
+    order = order[1:]
+    PARTS = ((0, 16, (3, 5, 6)), (16, 16, (0, 1, 2, 4)))
 
     barrier = pltpu.get_barrier_semaphore()
     friends = [(d, 0, 0) for d in range(1, 8)]
@@ -306,35 +321,35 @@
             copy.start()
         return copies
 
-    far = {0: 0, 1: 1, 2: 1, 3: 2, 4: 2, 5: 2, 6: 1, 7: 1}
-    order = [(a, b) for a in (0, 2) for b in range(8) if (a, b) != (0, 0)]
-
     def gather_second(k, first):
-        for copy in first:
-            copy.wait_recv()
-        W[k, 1, SLOT : SLOT + 32] = A[k]
         copies = {}
-        for a, b in order:
-            copies[a, b] = remote(
-                A.at[k], W.at[k, (1 - a) % 4, pl.ds(SLOT * ((1 - b) % 8), 32)], peer(0, a, b)
-            )
-        for a, b in sorted(order, key=lambda o: -far[o[1]]):
-            copies[a, b].start()
+        for part, (row, n, needed) in enumerate(PARTS):
+            for i in needed:
+                first[i].wait_recv()
+            W[k, 1, SLOT + row : SLOT + row + n] = A[k, row : row + n]
+            for o in reversed(order):
+                lo, hi, dy = o
+                rows = pl.ds(SLOT * lax.rem(1 - 2 * dy - hi * turn + 2 * GZ, GZ) + row, n)
+                device = (gx, lax.rem(gy + 2 * lo, GY), lax.rem(gz + 2 * dy + hi * turn + GZ, GZ))
+                copies[o, part] = remote(A.at[k, pl.ds(row, n)], W.at[k, (1 - 2 * lo) % GY, rows], device)
+                copies[o, part].start()
         return copies
 
     def gather_third(k, second):
         relays = []
 
-        def relay(a, b):
-            g, s = (1 - a) % 4, pl.ds(SLOT * ((1 - b) % 8), 32)
+        def relay(lo, hi, dy):
+            g = (1 - 2 * lo) % 4
+            s = pl.ds(SLOT * lax.rem(1 - 2 * dy + hi * turn + 2 * GZ, GZ), 32)
             to = lax.rem(g + 3 + 2 * core, 4)
             relays.append(remote(W.at[k, g, s], W.at[k, to, s], partner))
             relays[-1].start()
 
-        relay(0, 0)
-        for a, b in sorted(order, key=lambda o: far[o[1]]):
-            second[a, b].wait_recv()
-            relay(a, b)
+        relay(0, 0, 0)
+        for o in order:
+            for part in range(len(PARTS)):
+                second[o, part].wait_recv()
+            relay(*o)
         for copy in relays:
             copy.wait_recv()
         return relays
@@ -416,6 +431,10 @@
     d = [6.0 * w[k] + shift for k in range(3)]
     c = [jnp.max(DAMPING / jnp.full((8, 128), d[k], jnp.float32)) for k in range(3)]
 
+    ends = mm2(src[...].reshape(256, 128), mats[PACK]).reshape(16, 2, 8, 128)
+    spot = lax.div(lanes((16, 8, 128)), 16) == lax.broadcasted_iota(jnp.int32, (16, 8, 128), 1)
+    for y in range(2):
+        PK[y] = jnp.sum(jnp.where(spot, ends[:, y], 0.0), axis=1)
     pl.semaphore_wait(barrier, len(friends))
     pending = []
     first = gather_first(0)
@@ -424,7 +443,7 @@
     for dy, k in ((1, 0), (3, 1)):
         side.append(remote(f1o, LR1.at[k], peer(0, dy, 0)))
     for dy, k in ((1, 0), (3, 1)):
-        side.append(remote(src, LR0.at[k], peer(0, dy, 0)))
+        side.append(remote(PK, LR0.at[k], peer(0, dy, 0)))
     for copy in side:
         copy.start()
     pending += side
@@ -443,10 +462,13 @@
     corner1 = []
     around = [(1, 0), (-1, 0), (0, 1), (0, -1), (1, 1), (1, -1), (-1, 1), (-1, -1)]
     for dx, dz in around:
+        (n_x, from_x, to_x), (n_y, from_y, to_y) = (
+            {0: (8, 8, 8), 1: (6, 10, 2), -1: (6, 8, 16)}[step] for step in (dx, dz)
+        )
         corner1.append(
             remote(
-                F1.at[pl.ds(8, 8), pl.ds(8, 8)],
-                F1.at[pl.ds(8 - 8 * dx, 8), pl.ds(8 - 8 * dz, 8)],
+                F1.at[pl.ds(from_x, n_x), pl.ds(from_y, n_y)],
+                F1.at[pl.ds(to_x, n_x), pl.ds(to_y, n_y)],
                 peer(dx, 0, dz),
             )
         )
@@ -457,32 +479,35 @@
     side[2].wait_recv()
     side[3].wait_recv()
 
-    def halo0(i):
-        lane = lanes((16, 128))
-        H0[i] = jnp.where(lane < 8, LR0[1, i], jnp.where(lane >= 120, LR0[0, i], 0.0))
-        F0M[i + 6, 8:24] = src[i]
-        F0H[i + 6, 8:24] = H0[i]
-
-    loop(0, 16, halo0, 2)
+    after = lax.rem(lanes((2, 16, 128)), 16) < 8
+    HP[1:3, 6:22] = jnp.where(after, LR0[1], LR0[0])
+    F0M[6:22, 8:24] = src[...]
 
     third = gather_third(0, second)
     pending += third
 
-    corner0 = []
+    corner0, packed0 = [], []
     for dx, dz in around:
-        n_x, from_x, to_x = {0: (16, 0, 6), 1: (6, 10, 0), -1: (6, 0, 22)}[dx]
-        n_y, from_y, to_y = {0: (16, 0, 8), 1: (8, 8, 0), -1: (8, 0, 24)}[dz]
-        for source, target in ((src, F0M), (H0, F0H)):
-            corner0.append(
-                remote(
-                    source.at[pl.ds(from_x, n_x), pl.ds(from_y, n_y)],
-                    target.at[pl.ds(to_x, n_x), pl.ds(to_y, n_y)],
-                    peer(dx, 0, dz),
-                )
+        n_x, from_x, to_x = {0: (16, 0, 6), 1: (5, 11, 1), -1: (5, 0, 22)}[dx]
+        n_y, from_y, to_y = {0: (16, 0, 8), 1: (6, 10, 2), -1: (6, 0, 24)}[dz]
+        corner0.append(
+            remote(
+                src.at[pl.ds(from_x, n_x), pl.ds(from_y, n_y)],
+                F0M.at[pl.ds(to_x, n_x), pl.ds(to_y, n_y)],
+                peer(dx, 0, dz),
             )
-    for copy in corner0:
+        )
+        n_g, from_g, to_g = {0: (2, 1, 1), 1: (1, 2, 0), -1: (1, 1, 3)}[dz]
+        packed0.append(
+            remote(
+                HP.at[pl.ds(from_g, n_g), pl.ds(from_x + 6, n_x)],
+                HP.at[pl.ds(to_g, n_g), pl.ds(to_x, n_x)],
+                peer(dx, 0, dz),
+            )
+        )
+    for copy in packed0 + corner0:
         copy.start()
-    pending += corner0
+    pending += packed0 + corner0
 
     unpack(0)
     loads[1].wait()
@@ -509,7 +534,7 @@
         mid, s = beside1(lambda k: B1[k, 0:24], i)
         V1[i] = mid + c[1] * defect_of(mid, s, F1[i], 1)
 
-    loop(1, 23, pre1, 11)
+    loop(2, 22, pre1, 10)
 
     def res1(i):
         mid, s = beside1(lambda k: V1[k], i)
@@ -519,6 +544,16 @@
     restrict12(T1, 8)
     first = gather_first(1)
     second = gather_second(1, first)
+    for copy in packed0:
+        copy.wait_recv()
+
+    def open0(i):
+        spot = lax.div(lanes((4, 8, 128)), 16) == lax.broadcasted_iota(jnp.int32, (4, 8, 128), 1)
+        rows = jnp.where(spot, jnp.broadcast_to(HP[:, i].reshape(4, 1, 128), (4, 8, 128)), 0.0)
+        BH[i, 0:32] = rows.reshape(32, 128)
+
+    loop(1, 27, open0, 2)
+    F0H[1:27, 0:32] = mm2(BH[1:27, 0:32].reshape(832, 128), mats[OPEN]).reshape(26, 32, 128)
     third = gather_third(1, second)
     pending += first + list(second.values()) + third
     unpack(1)
@@ -645,15 +680,16 @@
     scratch = [
         pltpu.SMEM((1,), f32),
         vmem((16, 16, 128), f32),
-        vmem((15, 128, 128), jnp.bfloat16),
+        vmem((17, 128, 128), jnp.bfloat16),
         vmem((4, 256, 256), jnp.bfloat16),
         vmem((256, 128), f32),
         vmem((3, 32, 128), f32),
         vmem((3, 4, 8 * SLOT, 128), f32),
         vmem((8, 8, 128), f32),
         vmem((2, 8, 8, 128), f32),
-        vmem((2, 16, 16, 128), f32),
-        vmem((16, 16, 128), f32),
+        vmem((2, 2, 16, 128), f32),
+        vmem((2, 16, 128), f32),
+        vmem((4, 28, 128), f32),
         vmem((24, 24, 128), f32),
         vmem((28, 40, 128), f32),
         vmem((28, 40, 128), f32),

time: 67.9 us -> 63.9 us (0.941)
  Pallas kernels: 65.6 us -> 61.5 us
    pallas_call x1, Pallas kernels: 65.6 us -> 61.5 us  [step(): pl.pallas_call(kernel, out_shape=jax.ShapeDtypeStruct(source.shape, f32),...]
where the time goes in v3:
time: 63.9 us; the launch traced here: 63.7 us
  Pallas kernels  61.5 us (96%)
  local copies, waits for them, and re-layouts  1.57 us (2%)
  between operations  0.66 us (1%)
    pallas_call x1, Pallas kernels, step(): pl.pallas_call(kernel, out_shape=jax.ShapeDtypeStruct(source.shape, f32),...  61.5 us
    unnamed x1, local copies, waits for them, and re-layouts  1.57 us

profile of v3, /device:TPU:1, one launch (start us, length us, event | category | flops | bytes accessed | tf_op | source)
XLA Modules:
  0.0 63.7 jit_solution(1494773896634289131)
XLA Ops:
  0.7 61.5 %fcycle.1 = f32[16,16,128]{2,1,0:T(8,128)} custom-call(f32[1]{0:T(128)S(6)} %copy.7.shift_hbm, f32[16,16,128]{2,1,0:T(8,128)} %src_hbm.1, bf16[17,128,128]{2,1,0:T(8,128)(2,1)} %constant.6.clone.mats_hbm, bf16[4,256,256]{2,1,0:T(8,128)(2,1)} %constant.7.clone.hxy_hbm, f32[256,128]{1,0:T(8,128)} %constant.8.clone.lam_hbm), custom_call_target="tpu_custom_call" | custom-call | tf_op jit(solution)/shard_map/fcycle/pallas_call | solution.py:725
  62.2 1.6 %copy.8 = f32[16,16,128]{2,1,0:T(8,128)} copy(f32[16,16,128]{2,1,0:T(8,128)} %fcycle.1) | data formatting | bytes 262144

commit v4 on v3

--- a/solution.py
+++ b/solution.py
@@ -245,14 +245,14 @@
             mid, sums = beside2(V2, i, 4)
             keep3([G2[j, pl.ds(i + 1, 4)] - (d[2] * mid[j] - w[2] * sums[j]) for j in range(4)], t)
 
-        loop(0, 8, body, 4)
+        loop(0, 8, body, 8)
 
     def defect2_zero():
         def body(t):
             mid, sums = beside2(G2, 4 * t, 4)
             keep3([mid[j] - c[2] * (d[2] * mid[j] - w[2] * sums[j]) for j in range(4)], t)
 
-        loop(0, 8, body, 4)
+        loop(0, 8, body, 8)
 
     def solve3(t, weights, start, stop):
         x = T3[...].reshape(256, 128)
@@ -369,13 +369,14 @@
             for j in range(4):
                 G2[j, x + 1] = rows[j]
 
-        loop(0, 32, body, 16)
+        loop(0, 32, body, 32)
         wrap(G2)
 
-    def refine21(table, weights):
+    def refine21_z(table):
         x = U2[:, 3:19].reshape(512, 128)
         TZ2[...] = mm2(x, mats[table]).reshape(4, 16, 8, 128)
 
+    def refine21(weights, start, stop):
         def body(t):
             for p in range(2):
                 planes = [weighted(weights[p], lambda off: TZ2[j, t + 2 + off]) for j in range(4)]
@@ -388,7 +389,7 @@
 
                         B1[2 * t + p, pl.ds(2 * j + q, 4, stride=8), :] = weighted(weights[q], y_at)[0:4]
 
-        loop(0, 12, body, 3)
+        loop(start, stop, body, min(6, stop - start))
 
     def beside1(get, i):
         mid = get(i)
@@ -526,7 +527,8 @@
     defect2()
     correct2(False)
 
-    refine21(QZ21, CUBIC)
+    refine21_z(QZ21)
+    refine21(CUBIC, 3, 9)
     for copy in corner1:
         copy.wait_recv()
 
@@ -534,7 +536,7 @@
         mid, s = beside1(lambda k: B1[k, 0:24], i)
         V1[i] = mid + c[1] * defect_of(mid, s, F1[i], 1)
 
-    loop(2, 22, pre1, 10)
+    loop(7, 17, pre1, 10)
 
     def res1(i):
         mid, s = beside1(lambda k: V1[k], i)
@@ -544,6 +546,10 @@
     restrict12(T1, 8)
     first = gather_first(1)
     second = gather_second(1, first)
+    refine21(CUBIC, 0, 3)
+    refine21(CUBIC, 9, 12)
+    loop(2, 7, pre1, 5)
+    loop(17, 22, pre1, 5)
     for copy in packed0:
         copy.wait_recv()
 
@@ -558,7 +564,8 @@
     pending += first + list(second.values()) + third
     unpack(1)
     cycle2_zero()
-    refine21(PZ21, LINEAR)
+    refine21_z(PZ21)
+    refine21(LINEAR, 0, 12)
 
     def add1(i):
         V1[i] = V1[i] + B1[i, 0:24]
@@ -583,7 +590,7 @@
                 for q in range(2):
                     target[2 * t + p, pl.ds(q, 16, stride=2), :] = weighted(CUBIC[q], at.__getitem__)
 
-    loop(0, 14, cubic0, 2)
+    loop(1, 13, cubic0, 6)
     for copy in corner0:
         copy.wait_recv()
 
@@ -599,7 +606,7 @@
             s = s + jnp.where(lane == 127, up[1 - k], up[k]) + jnp.where(lane == 0, down[1 - k], down[k])
             v[i, 0:32] = mid[k] + c[0] * defect_of(mid[k], s, f[i, 0:32], 0)
 
-    loop(1, 27, pre0, 13)
+    loop(3, 25, pre0, 22)
 
     def res0(t):
         for a in range(2):
@@ -611,15 +618,15 @@
         for source, target in ((TM, RM), (TH, RHH)):
             target[t, 0:16] = source[t, pl.ds(0, 16, stride=2), :] + source[t, pl.ds(1, 16, stride=2), :]
 
-    loop(0, 12, res0, 6)
-    R1[:, 0:16] = (
-        mm2(RM[:, 0:16].reshape(192, 128), mats[RZ1]) + mm2(RHH[:, 0:16].reshape(192, 128), mats[RH])
-    ).reshape(12, 16, 128)
+    loop(1, 11, res0, 10)
+    R1[1:11, 0:16] = (
+        mm2(RM[1:11, 0:16].reshape(160, 128), mats[RZ1]) + mm2(RHH[1:11, 0:16].reshape(160, 128), mats[RH])
+    ).reshape(10, 16, 128)
 
     def zero1(i):
         D1[i, 0:16] = c[1] * R1[i, 0:16]
 
-    loop(0, 12, zero1, 4)
+    loop(1, 11, zero1, 5)
 
     def res1b(i):
         mid, s = beside1(lambda k: D1[k, 0:16], i)
@@ -629,11 +636,20 @@
     restrict12(T1, 4)
     first = gather_first(2)
     second = gather_second(2, first)
+    for t in (0, 13):
+        cubic0(t)
+    for i in (1, 2, 25, 26):
+        pre0(i)
+    for t in (0, 11):
+        res0(t)
+        R1[t, 0:16] = mm2(RM[t, 0:16], mats[RZ1]) + mm2(RHH[t, 0:16], mats[RH])
+        zero1(t)
     third = gather_third(2, second)
     pending += first + list(second.values()) + third
     unpack(2)
     cycle2_zero()
-    refine21(PZ21, LINEAR)
+    refine21_z(PZ21)
+    refine21(LINEAR, 3, 9)
 
     def add1b(i):
         D1[i, 0:16] = D1[i, 0:16] + B1[i + 6, 4:20]
@@ -661,14 +677,14 @@
                     target[i, pl.ds(q, 16, stride=2), :] = weighted(LINEAR[q], lambda off: roll(plane, -off, 0))
                 v[i, 0:32] = v[i, 0:32] + target[i, 0:32]
 
-    loop(0, 10, linear0, 2)
+    loop(0, 10, linear0, 5)
 
     def post0(i):
         mid, sums = beside0(i)
         v = mid[0] + c[0] * defect_of(mid[0], sums[0], F0M[i, 0:32], 0)
         out[i - 6] = v[8:24]
 
-    loop(6, 22, post0, 8)
+    loop(6, 22, post0, 16)
     for copy in pending:
         copy.wait_send()
 

time: 63.9 us -> 61.8 us (0.967)
  Pallas kernels: 61.5 us -> 59.5 us
    pallas_call x1, Pallas kernels: 61.5 us -> 59.5 us  [step(): pl.pallas_call(kernel, out_shape=jax.ShapeDtypeStruct(source.shape, f32),...]
where the time goes in v4:
time: 61.8 us; the launch traced here: 61.7 us
  Pallas kernels  59.5 us (96%)
  local copies, waits for them, and re-layouts  1.57 us (3%)
  between operations  0.66 us (1%)
    pallas_call x1, Pallas kernels, step(): pl.pallas_call(kernel, out_shape=jax.ShapeDtypeStruct(source.shape, f32),...  59.5 us
    unnamed x1, local copies, waits for them, and re-layouts  1.57 us

profile of v4, /device:TPU:1, one launch (start us, length us, event | category | flops | bytes accessed | tf_op | source)
XLA Modules:
  0.0 61.7 jit_solution(4823580015780140537)
XLA Ops:
  0.7 59.5 %fcycle.1 = f32[16,16,128]{2,1,0:T(8,128)} custom-call(f32[1]{0:T(128)S(6)} %copy.7.shift_hbm, f32[16,16,128]{2,1,0:T(8,128)} %src_hbm.1, bf16[17,128,128]{2,1,0:T(8,128)(2,1)} %constant.6.clone.mats_hbm, bf16[4,256,256]{2,1,0:T(8,128)(2,1)} %constant.7.clone.hxy_hbm, f32[256,128]{1,0:T(8,128)} %constant.8.clone.lam_hbm), custom_call_target="tpu_custom_call" | custom-call | tf_op jit(solution)/shard_map/fcycle/pallas_call | solution.py:741
  60.1 1.6 %copy.8 = f32[16,16,128]{2,1,0:T(8,128)} copy(f32[16,16,128]{2,1,0:T(8,128)} %fcycle.1) | data formatting | bytes 262144

commit v5 on v4

--- a/solution.py
+++ b/solution.py
@@ -305,11 +305,11 @@
                     part = source[2 * x + a, pl.ds(row + b, 4, stride=2), :]
                     s = part if s is None else s + part
             tmp[4 * x : 4 * x + 4] = s
-        z = mm2(tmp[...], mats[RZ2])
+        z = mm2(tmp[0:16], mats[RZ2])
         row_of = lax.broadcasted_iota(jnp.int32, (16, 128), 0)
         z = jnp.where(lax.div(lanes((16, 128)), 32) == lax.rem(row_of, 4), z, 0.0)
         z = z + roll(z, -1, 0)
-        tmp[...] = z + roll(z, -2, 0)
+        tmp[0:16] = z + roll(z, -2, 0)
 
     def gather_first(k):
         A[k, 8:12] = tmp[pl.ds(0, 4, stride=4), :]
@@ -424,7 +424,7 @@
                 part = src[2 * x + a, pl.ds(b, 8, stride=2), :]
                 s = part if s is None else s + part
         rows.append(s)
-    f1o[...] = mm2(jnp.concatenate(rows, axis=0), mats[RZ1]).reshape(8, 8, 128)
+    f1o[0:8] = mm2(jnp.concatenate(rows, axis=0), mats[RZ1]).reshape(8, 8, 128)
     restrict12(f1o, 0)
     inputs[1].wait()
     shift = shift_ref[0]
@@ -442,7 +442,7 @@
     pending += first
     side = []
     for dy, k in ((1, 0), (3, 1)):
-        side.append(remote(f1o, LR1.at[k], peer(0, dy, 0)))
+        side.append(remote(f1o.at[pl.ds(0, 8)], LR1.at[k], peer(0, dy, 0)))
     for dy, k in ((1, 0), (3, 1)):
         side.append(remote(PK, LR0.at[k], peer(0, dy, 0)))
     for copy in side:
@@ -458,7 +458,7 @@
     F1[8:16, 8:16] = jnp.where(
         lane < 8,
         roll(LR1[0], 64, 2),
-        jnp.where(lane < 72, f1o[...], jnp.where(lane < 80, roll(LR1[1], 64, 2), 0.0)),
+        jnp.where(lane < 72, f1o[0:8], jnp.where(lane < 80, roll(LR1[1], 64, 2), 0.0)),
     )
     corner1 = []
     around = [(1, 0), (-1, 0), (0, 1), (0, -1), (1, 1), (1, -1), (-1, 1), (-1, -1)]
@@ -701,11 +701,11 @@
         vmem((256, 128), f32),
         vmem((3, 32, 128), f32),
         vmem((3, 4, 8 * SLOT, 128), f32),
-        vmem((8, 8, 128), f32),
+        vmem((10, 8, 128), f32),
         vmem((2, 8, 8, 128), f32),
         vmem((2, 2, 16, 128), f32),
         vmem((2, 16, 128), f32),
-        vmem((4, 28, 128), f32),
+        vmem((4, 40, 128), f32),
         vmem((24, 24, 128), f32),
         vmem((28, 40, 128), f32),
         vmem((28, 40, 128), f32),
@@ -714,11 +714,11 @@
         vmem((4, 34, 8, 128), f32),
         vmem((2, 16, 8, 128), f32),
         vmem((4, 16, 8, 128), f32),
-        vmem((24, 40, 128), f32),
+        vmem((26, 40, 128), f32),
         vmem((24, 24, 128), f32),
         vmem((18, 24, 128), f32),
-        vmem((8, 24, 128), f32),
-        vmem((16, 128), f32),
+        vmem((9, 24, 128), f32),
+        vmem((48, 128), f32),
         vmem((18, 24, 128), f32),
         vmem((18, 24, 128), f32),
         vmem((28, 40, 128), f32),

time: 61.8 us -> 61.8 us (level)
  no operation moved by 1% of the time
where the time goes in v5:
time: 61.8 us; the launch traced here: 61.7 us
  Pallas kernels  59.5 us (96%)
  local copies, waits for them, and re-layouts  1.57 us (3%)
  between operations  0.66 us (1%)
    pallas_call x1, Pallas kernels, step(): pl.pallas_call(kernel, out_shape=jax.ShapeDtypeStruct(source.shape, f32),...  59.5 us
    unnamed x1, local copies, waits for them, and re-layouts  1.57 us

profile of v5, /device:TPU:1, one launch (start us, length us, event | category | flops | bytes accessed | tf_op | source)
XLA Modules:
  0.0 61.7 jit_solution(4557799151799589967)
XLA Ops:
  0.7 59.5 %fcycle.1 = f32[16,16,128]{2,1,0:T(8,128)} custom-call(f32[1]{0:T(128)S(6)} %copy.7.shift_hbm, f32[16,16,128]{2,1,0:T(8,128)} %src_hbm.1, bf16[17,128,128]{2,1,0:T(8,128)(2,1)} %constant.6.clone.mats_hbm, bf16[4,256,256]{2,1,0:T(8,128)(2,1)} %constant.7.clone.hxy_hbm, f32[256,128]{1,0:T(8,128)} %constant.8.clone.lam_hbm), custom_call_target="tpu_custom_call" | custom-call | tf_op jit(solution)/shard_map/fcycle/pallas_call | solution.py:741
  60.1 1.6 %copy.8 = f32[16,16,128]{2,1,0:T(8,128)} copy(f32[16,16,128]{2,1,0:T(8,128)} %fcycle.1) | data formatting | bytes 262144
